TPU v7x, 256 devices: a 2x2x32 block of a 4x8x32 slice. The times are simulated.
256 devices in a mesh: groups: 4 (over x, y), gx: 32 (over z), gy: 2 (over core).
Axes of the slice: x: 2, y: 2, z: 32, core: 2. Of those that a mesh axis runs over, the one named last changes fastest.
The devices are a block of a 4x8x32 slice.
Arguments:
- field: float32 [256, 64, 2048], P(('groups', 'gx'), 'gy'), parts along dimension 0, may hold values from -6 to 6
- spectral: float32 [32, 32, 16, 2, 32, 32], P('gy', 'gx'), may hold values from -2.1213202 to 2.1213202
- conv_first: float32 [3, 3, 3, 32, 32], replicated, may hold values from -0.21875 to 0.21875
- conv_second: float32 [3, 3, 3, 32, 32], replicated, may hold values from -0.21875 to 0.21875
- bias: float32 [32], replicated, may hold values from -3 to 3
Outputs:
- block_output: float32 [256, 64, 2048], P(('groups', 'gx'), 'gy'), parts along dimension 0
There are 4 independent parts, one for each index of `groups`. A program takes and returns all parts, laid end to end along the dimension named above; an argument that names none is the same for every part. Nothing has to cross between parts.
All inputs are finite; a program needn't handle non-finite values.
Results may differ from a plain program's by a relative error of at most 0.000057.
Values sent between devices are 32-bit elements; how exact they have to be, the bound alone decides.
No kernel may reach another device: no remote copies, remote signals or barrier semaphores. Data moves between devices by JAX's collectives and lax.ppermute only.
A program may use at most 128 MiB of HBM per device.

v0:
```python
import math

import jax
import jax.numpy as jnp
from jax import lax
from jax.sharding import PartitionSpec as P

CH = 32
NZ = 64
MX = 32
MY = 32
MZ = 16


HIGHEST = lax.Precision.HIGHEST


def cut_along(value, dim, length):
    before, after = (value.shape[:dim], value.shape[dim + 1 :])
    return jnp.moveaxis(value.reshape(*before, length, -1, *after), dim, 0)


def sum_at_owner(value, axis, dim):
    parts = cut_along(value, dim, lax.axis_size(axis))
    arrived = lax.all_to_all(parts, axis, split_axis=0, concat_axis=0, tiled=True)
    return arrived.sum(axis=0)


def with_halo(cells, sides, width):
    for axis, dim in sides:
        count = lax.axis_size(axis)
        ends = count - 1
        head = lax.slice_in_dim(cells, 0, width, axis=dim)
        tail = lax.slice_in_dim(cells, cells.shape[dim] - width, cells.shape[dim], axis=dim)
        cells = jnp.concatenate(
            [
                lax.ppermute(tail, axis, [(i, (i + 1) % count) for i in range(ends)]),
                cells,
                lax.ppermute(head, axis, [((i + 1) % count, i) for i in range(ends)]),
            ],
            axis=dim,
        )
    return cells


def frequency(position, length, retained):
    return jnp.where(position < retained // 2, position, length - retained + position)


def angle_table(first_list, second_list, length):
    product = first_list[:, None] * second_list[None, :] % length
    angles = product.astype(jnp.float32) * (2.0 * math.pi / length)
    return (jnp.cos(angles), jnp.sin(angles))


def rotate_sum(cos_table, sin_table, values, pattern, direction_sign):
    real_part = values[:, :, 0]
    imag_part = values[:, :, 1]
    out_real = jnp.einsum(
        pattern, cos_table, real_part, precision=HIGHEST
    ) + direction_sign * jnp.einsum(pattern, sin_table, imag_part, precision=HIGHEST)
    out_imag = jnp.einsum(
        pattern, cos_table, imag_part, precision=HIGHEST
    ) - direction_sign * jnp.einsum(pattern, sin_table, real_part, precision=HIGHEST)
    return jnp.stack([out_real, out_imag], axis=2)


def convolve(padded, weight):
    extent_x = padded.shape[0] - 2
    extent_y = padded.shape[1] - 2
    volume = padded.reshape(padded.shape[0], padded.shape[1], NZ, CH)
    volume = jnp.pad(volume, ((0, 0), (0, 0), (1, 1), (0, 0)))
    kernel = weight.reshape(3, 3, 3 * CH, CH)

    def plane(start):
        slab = lax.dynamic_slice_in_dim(volume, start, 3, 0)
        accumulated = jnp.zeros((extent_y, NZ, CH), jnp.float32)
        for shift_x in range(3):
            for shift_y in range(3):
                windowed = slab[shift_x, shift_y : shift_y + extent_y]
                stacked = jnp.concatenate(
                    [windowed[:, shift_z : shift_z + NZ] for shift_z in range(3)], axis=2
                )
                accumulated = accumulated + jnp.einsum(
                    "yzi,io->yzo", stacked, kernel[shift_x, shift_y], precision=HIGHEST
                )
        return accumulated

    return lax.map(plane, jnp.arange(extent_x, dtype=jnp.int32))


def mode_mix(inputs, matrix):
    return jnp.einsum("bazi,bazio->bazo", inputs, matrix, precision=HIGHEST)


def body(field, spectral, conv_first, conv_second, bias):
    cells_x, cells_y, merged_width = field.shape
    devices_x = lax.axis_size("gx")
    devices_y = lax.axis_size("gy")
    extent_x = cells_x * devices_x
    extent_y = cells_y * devices_y
    owned_x = MX // devices_x
    owned_y = MY // devices_y
    y_places = lax.axis_index("gy") * cells_y + jnp.arange(cells_y, dtype=jnp.int32)
    mode_width = MZ * CH
    volume = field.reshape(cells_x, cells_y, NZ, CH)
    z_modes_index = jnp.arange(MZ, dtype=jnp.int32)
    z_cos, z_sin = angle_table(z_modes_index, jnp.arange(NZ, dtype=jnp.int32), NZ)
    z_real = jnp.einsum("xyzc,kz->xykc", volume, z_cos, precision=HIGHEST)
    z_imag = -jnp.einsum("xyzc,kz->xykc", volume, z_sin, precision=HIGHEST)
    z_spectrum = jnp.stack([z_real, z_imag], axis=2).reshape(cells_x, cells_y, 2, mode_width)
    cos_table, sin_table = angle_table(
        frequency(jnp.arange(MX, dtype=jnp.int32), extent_x, MX),
        jnp.arange(extent_x, dtype=jnp.int32),
        extent_x,
    )
    kept_modes = rotate_sum(
        cos_table,
        sin_table,
        lax.all_to_all(z_spectrum, "gx", split_axis=1, concat_axis=0, tiled=True),
        "kx,xym->kym",
        1.0,
    )
    x_modes = lax.all_to_all(kept_modes, "gx", split_axis=0, concat_axis=1, tiled=True)
    row_index = jnp.arange(owned_y * lax.axis_size("gy"), dtype=jnp.int32)
    cos_table, sin_table = angle_table(frequency(row_index, extent_y, MY), y_places, extent_y)
    all_modes = sum_at_owner(rotate_sum(cos_table, sin_table, x_modes, "ky,xym->kxm", 1.0), "gy", 0)
    complex_parts = all_modes.reshape(owned_y, owned_x, 2, MZ, CH)
    real_inputs = complex_parts[:, :, 0]
    imag_inputs = complex_parts[:, :, 1]
    weight_real = spectral[:, :, :, 0]
    weight_imag = spectral[:, :, :, 1]
    mixed_real = mode_mix(real_inputs, weight_real) - mode_mix(imag_inputs, weight_imag)
    mixed_imag = mode_mix(real_inputs, weight_imag) + mode_mix(imag_inputs, weight_real)
    mixed = jnp.stack([mixed_real, mixed_imag], axis=2).reshape(owned_y, owned_x, 2, mode_width)
    portion = lax.all_gather(mixed, "gy", axis=0, tiled=True)
    row_index = jnp.arange(portion.shape[0], dtype=jnp.int32)
    cos_table, sin_table = angle_table(y_places, frequency(row_index, extent_y, MY), extent_y)
    y_cells = rotate_sum(cos_table, sin_table, portion, "yk,kxm->xym", -1.0)
    cos_table, sin_table = angle_table(
        jnp.arange(extent_x, dtype=jnp.int32),
        frequency(jnp.arange(MX, dtype=jnp.int32), extent_x, MX),
        extent_x,
    )
    cell_lines = rotate_sum(
        cos_table,
        sin_table,
        lax.all_to_all(y_cells, "gx", split_axis=1, concat_axis=0, tiled=True),
        "xk,kym->xym",
        -1.0,
    )
    planes = lax.all_to_all(cell_lines, "gx", split_axis=0, concat_axis=1, tiled=True)
    z_weights = jnp.where(z_modes_index == 0, 1.0, 2.0).astype(jnp.float32) / (
        extent_x * extent_y * NZ
    )
    planes_split = planes.reshape(cells_x, cells_y, 2, MZ, CH)
    spectral_part = jnp.einsum(
        "xykc,kz->xyzc", planes_split[:, :, 0], z_cos * z_weights[:, None], precision=HIGHEST
    ) - jnp.einsum(
        "xykc,kz->xyzc", planes_split[:, :, 1], z_sin * z_weights[:, None], precision=HIGHEST
    )
    with_rim = with_halo(field, (("gx", 0), ("gy", 1)), 1)
    first_hidden = jax.nn.gelu(convolve(with_rim, conv_first), approximate=False).reshape(
        cells_x, cells_y, merged_width
    )
    hidden_block = with_halo(first_hidden, (("gx", 0), ("gy", 1)), 1)
    second_branch = convolve(hidden_block, conv_second)
    result = jax.nn.gelu(spectral_part + second_branch + bias, approximate=False)
    return result.reshape(cells_x, cells_y, merged_width)


def solution(mesh):
    in_specs = (
        P(("groups", "gx"), "gy", None),
        P("gy", "gx", None, None, None, None),
        P(),
        P(),
        P(),
    )
    out_specs = P(("groups", "gx"), "gy", None)
    return jax.shard_map(body, mesh=mesh, in_specs=in_specs, out_specs=out_specs, check_vma=False)
```

profile of v0, /device:TPU:37, one launch (start us, length us, event | category | flops | bytes accessed | tf_op | source)
XLA Modules:
  0.0 375.4 jit_solution(12207379852496944950)
XLA Ops:
  1.9 5.3 %collective-permute-start = (f32[1,32,2048]{2,1,0:T(8,128)}, f32[1,32,2048]{2,1,0:T(8,128)}, u32[]{:S(2)}, u32[]{:S(2)}) collective-permute-start(f32[1,32,2048]{2,1,0:T(8,128)} %get-tuple-element.204), channel_id=1, source_target_pairs={{0,2},{2,4},{4,6},{6,8},{8,10},{10,12},{12,14},{14,16},{16,18},{18... | collective-permute-start | bytes 786440 | tf_op jit(solution)/shard_map/ppermute | solution.py:37
  15.0 33.2 %all-to-all-start = ((f32[2,32,2,512]{3,2,0,1:T(2,128)}), f32[2,32,2,512]{3,2,0,1:T(2,128)}, u32[]{:S(2)}, u32[]{:S(2)}) async-start(f32[2,32,2,512]{3,2,0,1:T(2,128)} %pad_maximum_fusion.2), calls=%async_computation | async-start | bytes 524288 | tf_op jit(solution)/shard_map/all_to_all | solution.py:120
  49.4 3.4 collective-permute-start.3
  59.8 5.3 %pad.7 = f32[4,34,66,32]{3,2,0,1:T(8,128)} pad(f32[4,34,64,32]{3,2,0,1:T(8,128)} %reshape.215, f32[]{:T(128)} %constant.44.clone.1), padding=0_0x0_0x1_1x0_0 | pad | bytes 2263044 | tf_op jit(solution)/shard_map/jit(_pad)/pad | solution.py:72
  65.2 84.3 %while.20 = (s32[]{:T(128)}, f32[2,32,64,32]{2,3,1,0:T(8,128)S(1)}, s32[2]{0:T(128)S(1)}, f32[4,34,66,32]{3,2,0,1:T(8,128)}, f32[3,3,96,32]{2,3,1,0:T(8,128)S(1)...) while((s32[]{:T(128)}, f32[2,32,64,32]{2,3,1,0:T(8,128)S(1)}, s32[2]{0:T(128)S(1)}, ...), condition=%wide.region_2.3_spmd, body=%wide.region_1.2_spmd.sunk | while | flops 683540480 | bytes 54296804 | solution.py:89
  67.9 5.3 %dynamic-slice_bitcast_fusion.20 = (f32[32,66,32]{2,1,0:T(8,128)S(1)}, f32[32,66,32]{2,1,0:T(8,128)S(1)}, f32[32,66,32]{2,1,0:T(8,128)S(1)}, f32[32,66,32]{2,1,0...) fusion(f32[4,34,66,32]{3,2,0,1:T(8,128)} %get-tuple-element.442, ...), kind=kLoop, calls=%fused_computation.10.clone.1 | loop fusion | bytes 4866068 | tf_op jit(solution)/shard_map/while/body/eval_jaxpr/squeeze | solution.py:80
  77.4 3.1 convolution_add_fusion.32
  91.2 3.1 convolution_add_fusion.36
  98.1 3.1 convolution_add_fusion.38
  106.8 5.1 %dynamic-slice_bitcast_fusion.20 = (f32[32,66,32]{2,1,0:T(8,128)S(1)}, f32[32,66,32]{2,1,0:T(8,128)S(1)}, f32[32,66,32]{2,1,0:T(8,128)S(1)}, f32[32,66,32]{2,1,0...) fusion(f32[4,34,66,32]{3,2,0,1:T(8,128)} %get-tuple-element.442, ...), kind=kLoop, calls=%fused_computation.10.clone.1 | loop fusion | bytes 4866068 | tf_op jit(solution)/shard_map/while/body/eval_jaxpr/squeeze | solution.py:80
  136.8 3.1 convolution_add_fusion.38
  153.0 21.7 %all-to-all-start.1 = ((f32[32,1,2,512]{3,2,1,0:T(2,128)}), f32[32,1,2,512]{3,2,1,0:T(2,128)S(1)}, u32[]{:S(2)}, u32[]{:S(2)}) async-start(f32[32,1,2,512]{3,2,1,0:T(2,128)} %copy.30), calls=%async_computation.1 | async-start | bytes 262144 | tf_op jit(solution)/shard_map/all_to_all | solution.py:124
  178.6 3.4 collective-permute-start.4
  187.7 4.9 %collective-permute-done.4 = f32[1,32,2048]{2,1,0:T(8,128)} collective-permute-done((f32[1,32,2048]{2,1,0:T(8,128)S(1)}, f32[1,32,2048]{2,1,0:T(8,128)}, u32[]{:S(2)}, u32[]{:S(2)}) %collective-permute-start.4) | collective-permute-done | bytes 262176 | tf_op jit(solution)/shard_map/ppermute | solution.py:37
  193.6 10.6 %all-to-all-done.1 = f32[32,1,2,512]{3,2,1,0:T(2,128)S(1)} async-done(((f32[32,1,2,512]{3,2,1,0:T(2,128)}), f32[32,1,2,512]{3,2,1,0:T(2,128)S(1)}, u32[]{:S(2)}, u32[]{:S(2)}) %all-to-all-start.1) | async-done | bytes 131104 | tf_op jit(solution)/shard_map/all_to_all | solution.py:124
  205.6 6.3 %all_to_all.62 = f32[2,16,1,2,512]{4,1,3,2,0:T(8,128)S(1)} all-to-all(f32[2,16,1,2,512]{4,1,3,2,0:T(8,128)S(1)} %pad_maximum_fusion.5), channel_id=1, replica_groups=mesh['groups'=4,'gx'=32,'gy'=2] {'gy'}, dimensions={0} | all-to-all | bytes 262144 | tf_op jit(solution)/shard_map/all_to_all | solution.py:25
  212.1 5.2 %fusion.150 = f32[16,16,1,32]{3,2,1,0:T(1,128)S(1)} fusion(f32[16,16,32,1]{2,3,1,0:T(1,128)S(1)} %bitcast.393, f32[16,1,16,2,32,32]{5,4,3,2,1,0:T(8,128)} %param.10), kind=kOutput, calls=%fused_computation.184 | convolution fusion | flops 3145728 | bytes 4259840 | tf_op jit(solution)/shard_map/bazi,bazio->bazo/dot_general | solution.py:93
  217.3 5.2 %fusion.156 = f32[16,16,1,32]{3,2,1,0:T(1,128)S(1)} fusion(f32[16,16,32,1]{2,3,1,0:T(1,128)S(1)} %bitcast.394, f32[16,1,16,2,32,32]{5,4,3,2,1,0:T(8,128)} %param.10), kind=kOutput, calls=%fused_computation.190 | convolution fusion | flops 3145728 | bytes 4259840 | tf_op jit(solution)/shard_map/bazi,bazio->bazo/dot_general | solution.py:93
  222.5 5.2 %fusion.154 = f32[16,16,1,32]{3,2,1,0:T(1,128)S(1)} fusion(f32[16,16,32,1]{2,3,1,0:T(1,128)S(1)} %bitcast.391, f32[16,1,16,2,32,32]{5,4,3,2,1,0:T(8,128)} %param.10), kind=kOutput, calls=%fused_computation.188 | convolution fusion | flops 3145728 | bytes 4259840 | tf_op jit(solution)/shard_map/bazi,bazio->bazo/dot_general | solution.py:93
  227.7 5.2 %fusion.152 = f32[16,16,1,32]{3,2,1,0:T(1,128)S(1)} fusion(f32[16,16,32,1]{2,3,1,0:T(1,128)S(1)} %bitcast.392, f32[16,1,16,2,32,32]{5,4,3,2,1,0:T(8,128)} %param.10), kind=kOutput, calls=%fused_computation.186 | convolution fusion | flops 3145728 | bytes 4259840 | tf_op jit(solution)/shard_map/bazi,bazio->bazo/dot_general | solution.py:93
  237.4 9.4 %all-to-all-start.3 = ((f32[1,32,2,512]{3,2,0,1:T(2,128)}), f32[1,32,2,512]{3,2,0,1:T(2,128)S(1)}, u32[]{:S(2)}, u32[]{:S(2)}) async-start(f32[1,32,2,512]{3,2,0,1:T(2,128)} %copy.34), calls=%async_computation.3 | async-start | bytes 262144 | tf_op jit(solution)/shard_map/all_to_all | solution.py:148
  256.5 5.3 %pad.8 = f32[4,34,66,32]{3,2,0,1:T(8,128)} pad(f32[4,34,64,32]{3,2,0,1:T(8,128)} %reshape.218, f32[]{:T(128)} %constant.44.clone.1), padding=0_0x0_0x1_1x0_0 | pad | bytes 2263044 | tf_op jit(solution)/shard_map/jit(_pad)/pad | solution.py:72
  261.8 14.2 %all-to-all-done.3 = f32[1,32,2,512]{3,2,0,1:T(2,128)S(1)} async-done(((f32[1,32,2,512]{3,2,0,1:T(2,128)}), f32[1,32,2,512]{3,2,0,1:T(2,128)S(1)}, u32[]{:S(2)}, u32[]{:S(2)}) %all-to-all-start.3) | async-done | bytes 131104 | tf_op jit(solution)/shard_map/all_to_all | solution.py:148
  278.7 7.6 %all-to-all-start.4 = ((f32[64,1,2,512]{3,2,1,0:T(2,128)}), f32[64,1,2,512]{3,2,1,0:T(2,128)}, u32[]{:S(2)}, u32[]{:S(2)}) async-start(f32[64,1,2,512]{3,2,1,0:T(2,128)} %copy.35), calls=%async_computation.4 | async-start | bytes 524288 | tf_op jit(solution)/shard_map/all_to_all | solution.py:152
  286.4 78.0 %while.21 = (s32[]{:T(128)}, f32[2,32,64,32]{2,3,1,0:T(8,128)S(1)}, s32[2]{0:T(128)S(1)}, f32[4,34,66,32]{3,2,0,1:T(8,128)}, f32[3,3,96,32]{2,3,1,0:T(8,128)S(1)...) while((s32[]{:T(128)}, f32[2,32,64,32]{2,3,1,0:T(8,128)S(1)}, s32[2]{0:T(128)S(1)}, ...), condition=%wide.region_4.5_spmd, body=%wide.region_3.4_spmd.sunk | while | flops 683540480 | bytes 54296804 | solution.py:89
  289.0 5.3 %dynamic-slice_bitcast_fusion.21 = (f32[32,66,32]{2,1,0:T(8,128)S(1)}, f32[32,66,32]{2,1,0:T(8,128)S(1)}, f32[32,66,32]{2,1,0:T(8,128)S(1)}, f32[32,66,32]{2,1,0...) fusion(f32[4,34,66,32]{3,2,0,1:T(8,128)} %get-tuple-element.472, ...), kind=kLoop, calls=%fused_computation.102.clone.1 | loop fusion | bytes 4866068 | tf_op jit(solution)/shard_map/while/body/eval_jaxpr/squeeze | solution.py:80
  319.2 3.1 convolution_add_fusion.45
  327.9 5.1 %dynamic-slice_bitcast_fusion.21 = (f32[32,66,32]{2,1,0:T(8,128)S(1)}, f32[32,66,32]{2,1,0:T(8,128)S(1)}, f32[32,66,32]{2,1,0:T(8,128)S(1)}, f32[32,66,32]{2,1,0...) fusion(f32[4,34,66,32]{3,2,0,1:T(8,128)} %get-tuple-element.472, ...), kind=kLoop, calls=%fused_computation.102.clone.1 | loop fusion | bytes 4866068 | tf_op jit(solution)/shard_map/while/body/eval_jaxpr/squeeze | solution.py:80
  337.2 3.1 convolution_add_fusion.39
  344.1 3.1 convolution_add_fusion.41
  357.9 3.1 convolution_add_fusion.45
  368.6 4.1 %fusion.179 = f32[2,32,64,32]{2,3,1,0:T(8,128)S(1)} fusion(f32[2,32,64,32]{2,3,1,0:T(8,128)S(1)} %copy-done.3, f32[64,2,32,32]{0,3,2,1:T(8,128)S(1)} %fusion.194, f32[2,32,2,16,32]{4,3,1,0,2:T(8,128)S(1)} %reshape.214, f32[32]{0:T(128)S(1)} %copy-done.8, f32[16]{0:T(128)S(1)} %copy-done.7), kind=kOutput, calls=%fused_computation.228 | convolution fusion | flops 33963008 | bytes 3146752 | tf_op jit(solution)/shard_map/xykc,kz->xyzc/dot_general | solution.py:159
  (164 shorter events, 158.1 us)
Async XLA Ops:
  0.0 8.5 %copy-start = (f32[2,32,2048]{2,1,0:T(8,128)S(1)}, f32[2,32,2048]{2,1,0:T(8,128)}, u32[]{:S(2)}) copy-start(f32[2,32,2048]{2,1,0:T(8,128)} %param.9) | copy-start | bytes 1572868
  1.9 46.3 %collective-permute-start = (f32[1,32,2048]{2,1,0:T(8,128)}, f32[1,32,2048]{2,1,0:T(8,128)}, u32[]{:S(2)}, u32[]{:S(2)}) collective-permute-start(f32[1,32,2048]{2,1,0:T(8,128)} %get-tuple-element.204), channel_id=1, source_target_pairs={{0,2},{2,4},{4,6},{6,8},{8,10},{10,12},{12,14},{14,16},{16,18},{18... | collective-permute-start | bytes 786440 | tf_op jit(solution)/shard_map/ppermute | solution.py:37
  7.2 42.0 %collective-permute-start.1 = (f32[1,32,2048]{2,1,0:T(8,128)}, f32[1,32,2048]{2,1,0:T(8,128)S(1)}, u32[]{:S(2)}, u32[]{:S(2)}) collective-permute-start(f32[1,32,2048]{2,1,0:T(8,128)} %get-tuple-element.203), channel_id=1, source_target_pairs={{2,0},{4,2},{6,4},{8,6},{10,8},{12,10},{14,12},{16,14},{18,16},{20... | collective-permute-start | bytes 786440 | tf_op jit(solution)/shard_map/ppermute | solution.py:39
  15.0 134.6 %all-to-all-start = ((f32[2,32,2,512]{3,2,0,1:T(2,128)}), f32[2,32,2,512]{3,2,0,1:T(2,128)}, u32[]{:S(2)}, u32[]{:S(2)}) async-start(f32[2,32,2,512]{3,2,0,1:T(2,128)} %pad_maximum_fusion.2), calls=%async_computation | async-start | bytes 524288 | tf_op jit(solution)/shard_map/all_to_all | solution.py:120
  48.2 6.5 %copy-start.4 = (f32[3,3,3,32,32]{4,3,2,1,0:T(8,128)S(1)}, f32[3,3,3,32,32]{4,3,2,1,0:T(8,128)}, u32[]{:S(2)}) copy-start(f32[3,3,3,32,32]{4,3,2,1,0:T(8,128)} %param.11) | copy-start | bytes 331780
  49.4 5.5 %collective-permute-start.3 = (f32[4,1,2048]{2,1,0:T(1,128)S(1)}, f32[4,1,2048]{2,1,0:T(1,128)S(1)}, u32[]{:S(2)}, u32[]{:S(2)}) collective-permute-start(f32[4,1,2048]{2,1,0:T(1,128)S(1)} %get-tuple-element.202), channel_id=1, source_target_pairs={{1,0},{3,2},{5,4},{7,6},{9,8},{11,10},{13,12},{15,14},{17,16},{19,... | collective-permute-start | bytes 98312 | tf_op jit(solution)/shard_map/ppermute | solution.py:39
  52.8 3.1 collective-permute-start.2
  65.2 85.6 %copy-start.6 = (s32[32]{0:T(128)S(1)}, s32[32]{0:T(128)}, u32[]{:S(2)}) copy-start(s32[32]{0:T(128)} %compare_select_fusion) | copy-start | bytes 388
  153.0 51.2 %all-to-all-start.1 = ((f32[32,1,2,512]{3,2,1,0:T(2,128)}), f32[32,1,2,512]{3,2,1,0:T(2,128)S(1)}, u32[]{:S(2)}, u32[]{:S(2)}) async-start(f32[32,1,2,512]{3,2,1,0:T(2,128)} %copy.30), calls=%async_computation.1 | async-start | bytes 262144 | tf_op jit(solution)/shard_map/all_to_all | solution.py:124
  178.6 13.9 %collective-permute-start.4 = (f32[1,32,2048]{2,1,0:T(8,128)S(1)}, f32[1,32,2048]{2,1,0:T(8,128)}, u32[]{:S(2)}, u32[]{:S(2)}) collective-permute-start(f32[1,32,2048]{2,1,0:T(8,128)S(1)} %slice.361), channel_id=1, source_target_pairs={{0,2},{2,4},{4,6},{6,8},{8,10},{10,12},{12,14},{14,16},{16,18},{18... | collective-permute-start | bytes 786440 | tf_op jit(solution)/shard_map/ppermute | solution.py:37
  185.9 7.7 %copy-start.1 = (f32[2,32,2048]{2,1,0:T(8,128)S(1)}, f32[2,32,2048]{2,1,0:T(8,128)}, u32[]{:S(2)}) copy-start(f32[2,32,2048]{2,1,0:T(8,128)} %reshape.217) | copy-start | bytes 1572868
  186.4 60.5 %collective-permute-start.5 = (f32[1,32,2048]{2,1,0:T(8,128)S(1)}, f32[1,32,2048]{2,1,0:T(8,128)S(1)}, u32[]{:S(2)}, u32[]{:S(2)}) collective-permute-start(f32[1,32,2048]{2,1,0:T(8,128)S(1)} %slice.363), channel_id=1, source_target_pairs={{2,0},{4,2},{6,4},{8,6},{10,8},{12,10},{14,12},{16,14},{18,16},{20... | collective-permute-start | bytes 786440 | tf_op jit(solution)/shard_map/ppermute | solution.py:39
  233.2 18.2 %copy-start.5 = (f32[3,3,3,32,32]{4,3,2,1,0:T(8,128)S(1)}, f32[3,3,3,32,32]{4,3,2,1,0:T(8,128)}, u32[]{:S(2)}) copy-start(f32[3,3,3,32,32]{4,3,2,1,0:T(8,128)} %param.12) | copy-start | bytes 331780
  237.4 38.6 %all-to-all-start.3 = ((f32[1,32,2,512]{3,2,0,1:T(2,128)}), f32[1,32,2,512]{3,2,0,1:T(2,128)S(1)}, u32[]{:S(2)}, u32[]{:S(2)}) async-start(f32[1,32,2,512]{3,2,0,1:T(2,128)} %copy.34), calls=%async_computation.3 | async-start | bytes 262144 | tf_op jit(solution)/shard_map/all_to_all | solution.py:148
  246.9 4.7 %collective-permute-start.7 = (f32[4,1,2048]{2,1,0:T(1,128)S(1)}, f32[4,1,2048]{2,1,0:T(1,128)S(1)}, u32[]{:S(2)}, u32[]{:S(2)}) collective-permute-start(f32[4,1,2048]{2,1,0:T(1,128)S(1)} %get-tuple-element.198), channel_id=1, source_target_pairs={{1,0},{3,2},{5,4},{7,6},{9,8},{11,10},{13,12},{15,14},{17,16},{19,... | collective-permute-start | bytes 98312 | tf_op jit(solution)/shard_map/ppermute | solution.py:39
  249.5 3.1 collective-permute-start.6
  278.7 85.7 %all-to-all-start.4 = ((f32[64,1,2,512]{3,2,1,0:T(2,128)}), f32[64,1,2,512]{3,2,1,0:T(2,128)}, u32[]{:S(2)}, u32[]{:S(2)}) async-start(f32[64,1,2,512]{3,2,1,0:T(2,128)} %copy.35), calls=%async_computation.4 | async-start | bytes 524288 | tf_op jit(solution)/shard_map/all_to_all | solution.py:152
  364.4 1.0 copy-start.2
  364.4 2.3 copy-start.7
  366.4 2.2 copy-start.8
  366.7 1.9 copy-start.3
where the time goes:
time: 382 us; the launch traced here: 375 us
  matrix products  147 us (38%)
  starting transfers between devices  91.8 us (24%)
  local copies, waits for them, and re-layouts  75.2 us (20%)
  waiting for transfers between devices  31.8 us (8%)
  loops' own time  15 us (4%)
  blocking collectives  8.41 us (2%)
  other arithmetic  4.77 us (1%)
    dot_general x36, matrix products, plane(): jnp.einsum('yzi,io->yzo', stacked, kernel[shift_x, shift_y], precision=HI...  112 us
    all_to_all x1, starting transfers between devices, body(): lax.all_to_all(z_spectrum, 'gx', split_axis=1, concat_axis=0, tiled=True)  33.2 us
    all_to_all x1, starting transfers between devices, body(): lax.all_to_all(kept_modes, 'gx', split_axis=0, concat_axis=1, tiled=True)  21.7 us
    squeeze x4, local copies, waits for them, and re-layouts, plane(): windowed = slab[shift_x, shift_y:shift_y + extent_y]  20.9 us
    dot_general x4, matrix products, mode_mix(): return jnp.einsum('bazi,bazio->bazo', inputs, matrix, precision=HIGHEST)  20.8 us
    another operation x2, loops' own time, convolve(): return lax.map(plane, jnp.arange(extent_x, dtype=jnp.int32))  15 us
    all_to_all x1, waiting for transfers between devices, body(): lax.all_to_all(y_cells, 'gx', split_axis=1, concat_axis=0, tiled=True)  14.2 us
    slice x20, local copies, waits for them, and re-layouts, plane(): windowed[:, shift_z:shift_z + NZ]  11.9 us
  transfers between devices with their start and end apart: 12, of which 5 were waited for; matrix products, arithmetic and copies ran while one was open for 56% of the time, Pallas kernels for 0%

commit v1 on v0

v1 whole, which is shorter than its diff:
```python
import functools
import math

import jax
import jax.numpy as jnp
import numpy as np
from jax import lax
from jax.experimental import pallas as pl
from jax.experimental.pallas import tpu as pltpu
from jax.sharding import PartitionSpec as P

CH = 32
NZ = 64
MX = 32
MY = 32
MZ = 16

LANES = 128
GROUP = LANES // CH
ZQ = NZ // GROUP
ROWS = 8
F32 = jnp.float32
BF16 = jnp.bfloat16
VMEM = pl.BlockSpec(memory_space=pltpu.VMEM)


def small_grant():
    return pltpu.CompilerParams(vmem_limit_bytes=12 << 20)


def split(value):
    high = value.astype(BF16)
    return high, (value - high.astype(F32)).astype(BF16)


def host_split(table):
    table = np.asarray(table, np.float32)
    high = table.astype(jnp.bfloat16)
    low = (table - high.astype(np.float32)).astype(jnp.bfloat16)
    return np.stack([high, low])


def dot(a, b):
    return jnp.dot(a, b, preferred_element_type=F32)


def dot3(table_high, table_low, value):
    high, low = split(value)
    return dot(table_high, high) + (dot(table_low, high) + dot(table_high, low))


def gelu(v):
    return v * (1.0 + lax.erf(v * (1.0 / math.sqrt(2.0)))) * 0.5


def kept(count, length):
    return np.array([j if j < count // 2 else length - count + j for j in range(count)])


def rotation(angle):
    return np.array([[np.cos(angle), -np.sin(angle)], [np.sin(angle), np.cos(angle)]])


def forward_tables(cells_x, cells_y, devices_y):
    extent = cells_y * devices_y
    freq = kept(MY, extent)
    owned = MY // devices_y
    table = np.zeros((devices_y, devices_y, owned, cells_x, 2, 2, cells_x, cells_y))
    for g in range(devices_y):
        places = g * cells_y + np.arange(cells_y)
        for t in range(devices_y):
            rows = freq[t * owned : (t + 1) * owned]
            turn = rotation(-2 * np.pi * (rows[:, None] * places[None, :] % extent) / extent)
            for x in range(cells_x):
                table[g, t, :, x, :, :, x, :] = turn.transpose(2, 0, 1, 3)
    return table.reshape(devices_y, devices_y, owned * cells_x * 2, 2 * cells_x * cells_y)


def z_twiddle(sign):
    zr = np.repeat(np.arange(GROUP), CH)
    angle = sign * 2 * np.pi * np.arange(MZ)[:, None] * zr[None, :] / NZ
    return np.stack([np.cos(angle), np.sin(angle)]).astype(np.float32)


def z_forward(blocks, twiddle, lane):
    half = ZQ // 2
    even = [None] + [blocks[n] + blocks[ZQ - n] for n in range(1, half)]
    odd = [None] + [blocks[n] - blocks[ZQ - n] for n in range(1, half)]
    real, imag = [], []
    for k in range(half + 1):
        re = blocks[0] + blocks[half] if k % 2 == 0 else blocks[0] - blocks[half]
        im = None
        for n in range(1, half):
            c = math.cos(2 * math.pi * (k * n % ZQ) / ZQ)
            s = math.sin(2 * math.pi * (k * n % ZQ) / ZQ)
            if abs(c) > 1e-9:
                re = re + even[n] * c
            if abs(s) > 1e-9:
                im = odd[n] * -s if im is None else im - odd[n] * s
        real.append(re)
        imag.append(im)
    out = ([], [])
    upper = lane >= LANES // 2
    odd_group = (lane // CH) % 2 == 1
    for first in range(0, MZ, GROUP):
        pieces = ([], [])
        for k in range(first, first + GROUP):
            fold = k if k <= half else ZQ - k
            fr, fi = real[fold], imag[fold]
            if fi is not None and k > half:
                fi = -fi
            tc, ts = twiddle(k)
            if fi is None:
                pieces[0].append(fr * tc)
                pieces[1].append(fr * ts)
            else:
                pieces[0].append(fr * tc - fi * ts)
                pieces[1].append(fi * tc + fr * ts)
        for part in range(2):
            y0, y1, y2, y3 = pieces[part]
            a = jnp.where(upper, y2, y0) + pltpu.roll(jnp.where(upper, y0, y2), LANES // 2, 1)
            b = jnp.where(upper, y3, y1) + pltpu.roll(jnp.where(upper, y1, y3), LANES // 2, 1)
            out[part].append(
                jnp.where(odd_group, b + pltpu.roll(b, CH, 1), a + pltpu.roll(a, LANES - CH, 1))
            )
    return out


def forward_kernel(cells_ref, table_ref, twiddle_ref, keep_ref, send_ref, z_ref, *, devices_y):
    rows = cells_ref.shape[0]
    lane = lax.broadcasted_iota(jnp.int32, (ROWS, LANES), 1)

    def step(i, carry):
        start = pl.multiple_of(i * ROWS, ROWS)
        blocks = [cells_ref[pl.ds(start, ROWS), q * LANES : (q + 1) * LANES] for q in range(ZQ)]

        def twiddle(k):
            return (
                jnp.broadcast_to(twiddle_ref[0, k : k + 1, :], (ROWS, LANES)),
                jnp.broadcast_to(twiddle_ref[1, k : k + 1, :], (ROWS, LANES)),
            )

        real, imag = z_forward(blocks, twiddle, lane)
        for h in range(MZ // GROUP):
            z_ref[pl.ds(start, ROWS), h * LANES : (h + 1) * LANES] = real[h]
            z_ref[pl.ds(start + rows, ROWS), h * LANES : (h + 1) * LANES] = imag[h]
        return carry

    lax.fori_loop(0, rows // ROWS, step, 0)
    here = lax.axis_index("gy")
    there = devices_y - 1 - here
    high, low = split(z_ref[...])
    for target, out_ref in ((there, send_ref), (here, keep_ref)):
        table = table_ref[here, target, 0]
        modes = dot(table, high) + (dot(table_ref[here, target, 1], high) + dot(table, low))
        for h in range(MZ // GROUP):
            for kp in range(modes.shape[0] // ROWS):
                out_ref[kp * (MZ // GROUP) + h] = modes[
                    kp * ROWS : (kp + 1) * ROWS, h * LANES : (h + 1) * LANES
                ]


def x_tables(cells_x, devices_x, pair):
    extent = cells_x * devices_x
    freq = kept(MX, extent)
    place = np.arange(extent)
    forward = np.zeros((MX, pair, 2, devices_x, pair, cells_x, 2))
    inverse = np.zeros((devices_x, pair, cells_x, 2, MX, pair, 2))
    angle = 2 * np.pi * (freq[:, None] * place[None, :] % extent) / extent
    turn = rotation(-angle).reshape(2, 2, MX, devices_x, cells_x)
    back = rotation(angle).reshape(2, 2, MX, devices_x, cells_x)
    for q in range(pair):
        forward[:, q, :, :, q] = turn.transpose(2, 0, 3, 4, 1)
        inverse[:, q, :, :, :, q] = back.transpose(3, 4, 0, 2, 1)
    return (
        forward.reshape(MX * pair * 2, devices_x * pair * cells_x * 2),
        inverse.reshape(devices_x * pair * cells_x * 2, MX * pair * 2),
    )


def matrix_kernel(table_ref, value_ref, out_ref):
    out_ref[...] = dot3(table_ref[0], table_ref[1], value_ref[...])


def apply_matrix(table, value):
    return pl.pallas_call(
        matrix_kernel,
        out_shape=jax.ShapeDtypeStruct((table.shape[1], value.shape[1]), F32),
        in_specs=[VMEM, VMEM],
        out_specs=VMEM,
        compiler_params=small_grant(),
    )(table, value)


def mix_kernel(modes_ref, weight_ref, out_ref):
    count = modes_ref.shape[0] // 2
    halves = GROUP * count // LANES
    per = GROUP // halves
    parts = []
    for part in range(2):
        turned = modes_ref[pl.ds(part, count, stride=2), :].T
        parts.append(
            [
                jnp.concatenate(
                    [turned[(h * per + g) * CH : (h * per + g + 1) * CH] for g in range(per)],
                    axis=1,
                )
                for h in range(halves)
            ]
        )
    outs = ([], [])
    for h in range(halves):
        re, im = parts[0][h], parts[1][h]
        acc_re = jnp.zeros((CH, LANES), F32)
        acc_im = jnp.zeros((CH, LANES), F32)
        for c in range(CH):
            wr = weight_ref[0, h, c]
            wi = weight_ref[1, h, c]
            a = re[c : c + 1, :]
            b = im[c : c + 1, :]
            acc_re = acc_re + (a * wr - b * wi)
            acc_im = acc_im + (a * wi + b * wr)
        for g in range(per):
            outs[0].append(acc_re[:, g * count : (g + 1) * count])
            outs[1].append(acc_im[:, g * count : (g + 1) * count])
    for part in range(2):
        out_ref[pl.ds(part, count, stride=2), :] = jnp.concatenate(outs[part], axis=0).T


def inverse_tables(cells_x, cells_y, devices_y):
    extent = cells_y * devices_y
    freq = kept(MY, extent)
    owned = MY // devices_y
    table = np.zeros((devices_y, devices_y, 2, cells_x, cells_y, owned, cells_x, 2))
    for g in range(devices_y):
        places = g * cells_y + np.arange(cells_y)
        for t in range(devices_y):
            rows = freq[t * owned : (t + 1) * owned]
            turn = rotation(2 * np.pi * (places[:, None] * rows[None, :] % extent) / extent)
            for x in range(cells_x):
                table[g, t, :, x, :, :, x, :] = turn.transpose(0, 2, 3, 1)
    return table.reshape(devices_y, devices_y, 2 * cells_x * cells_y, owned * cells_x * 2)


def end_kernel(
    own_ref, other_ref, table_ref, twiddle_ref, branch_ref, bias_ref, out_ref, y_ref, *, devices_y
):
    here = lax.axis_index("gy")
    there = devices_y - 1 - here
    wide = MZ // GROUP
    rows = out_ref.shape[0]

    def gather(ref):
        pairs = ref.shape[0] // wide
        return jnp.concatenate(
            [
                jnp.concatenate([ref[kp * wide + h] for kp in range(pairs)], axis=0)
                for h in range(wide)
            ],
            axis=1,
        )

    y_ref[...] = dot3(table_ref[here, here, 0], table_ref[here, here, 1], gather(own_ref)) + dot3(
        table_ref[here, there, 0], table_ref[here, there, 1], gather(other_ref)
    )
    lane = lax.broadcasted_iota(jnp.int32, (ROWS, LANES), 1)
    group = lane // CH
    half = ZQ // 2

    def step(i, carry):
        start = pl.multiple_of(i * ROWS, ROWS)

        def spread(value, g):
            kept_lanes = jnp.where(group == g, value, 0.0)
            kept_lanes = kept_lanes + pltpu.roll(kept_lanes, LANES // 2, 1)
            return kept_lanes + pltpu.roll(kept_lanes, CH, 1)

        real, imag = [], []
        for k in range(MZ):
            h, g = divmod(k, GROUP)
            re = spread(y_ref[pl.ds(start, ROWS), h * LANES : (h + 1) * LANES], g)
            im = spread(y_ref[pl.ds(start + rows, ROWS), h * LANES : (h + 1) * LANES], g)
            tc = jnp.broadcast_to(twiddle_ref[0, k : k + 1, :], (ROWS, LANES))
            ts = jnp.broadcast_to(twiddle_ref[1, k : k + 1, :], (ROWS, LANES))
            real.append(re * tc - im * ts)
            imag.append(re * ts + im * tc)
        even = [None] + [real[k] + real[ZQ - k] for k in range(1, half)]
        odd = [None] + [imag[k] - imag[ZQ - k] for k in range(1, half)]
        bias = jnp.broadcast_to(bias_ref[...], (ROWS, LANES))
        for q in range(half + 1):
            cos_part = real[0] + real[half] if q % 2 == 0 else real[0] - real[half]
            cos_part = cos_part + bias
            sin_part = None
            for k in range(1, half):
                c = math.cos(2 * math.pi * (k * q % ZQ) / ZQ)
                s = math.sin(2 * math.pi * (k * q % ZQ) / ZQ)
                if abs(c) > 1e-9:
                    cos_part = cos_part + even[k] * c
                if abs(s) > 1e-9:
                    sin_part = odd[k] * s if sin_part is None else sin_part + odd[k] * s
            places = [(q, -1.0)] if sin_part is None else [(q, -1.0), (ZQ - q, 1.0)]
            for place, sign in places:
                value = cos_part
                if sin_part is not None:
                    value = cos_part + sin_part if sign > 0 else cos_part - sin_part
                lanes = slice(place * LANES, (place + 1) * LANES)
                value = value + branch_ref[pl.ds(start, ROWS), lanes]
                out_ref[pl.ds(start, ROWS), lanes] = gelu(value)
        return carry

    lax.fori_loop(0, rows // ROWS, step, 0)


BLOCK = 8
WINDOW = BLOCK + 2 * GROUP
TOP = 8


def conv_kernel(
    cells_ref, before_ref, after_ref, rim_ref, weight_ref, out_ref, pad_ref, high_ref, low_ref,
    table_high_ref, table_low_ref, acc_ref, *, activate,
):
    cells_x, cells_y, width = cells_ref.shape
    here = lax.axis_index("gy")
    blocks = NZ // BLOCK
    out_lanes = BLOCK * CH
    in_lanes = WINDOW * CH

    lane = lax.broadcasted_iota(jnp.int32, (CH, out_lanes), 1)
    group = lane // CH
    repeat = jnp.where(
        lax.broadcasted_iota(jnp.int32, (CH, out_lanes), 0) == lane % CH, 1.0, 0.0
    ).astype(BF16)
    zero = jnp.zeros((CH, out_lanes), BF16)

    def build(i, carry):
        for value, ref in zip(split(weight_ref[i]), (table_high_ref, table_low_ref), strict=True):
            wide = dot(value, repeat)
            for z in range(WINDOW):
                total = None
                for e in range(3):
                    place = z - (GROUP - 1) - e
                    if 0 <= place < BLOCK:
                        term = jnp.where(group == place, wide[e * CH : (e + 1) * CH], 0.0)
                        total = term if total is None else total + term
                ref[i, z * CH : (z + 1) * CH, :] = zero if total is None else total.astype(BF16)
        return carry

    lax.fori_loop(0, 9, build, 0)

    pad_ref[:, :, :LANES] = jnp.zeros((cells_x + 2, pad_ref.shape[1], LANES), F32)
    pad_ref[:, :, LANES + width :] = jnp.zeros((cells_x + 2, pad_ref.shape[1], LANES), F32)
    inner = slice(LANES, LANES + width)
    pad_ref[0, TOP : TOP + cells_y, inner] = before_ref[0]
    for x in range(cells_x):
        pad_ref[1 + x, TOP : TOP + cells_y, inner] = cells_ref[x]
    pad_ref[1 + cells_x, TOP : TOP + cells_y, inner] = after_ref[0]
    for x in range(cells_x + 2):
        row = rim_ref[x : x + 1, :]
        pad_ref[x, TOP - 1 : TOP, inner] = jnp.where(here == 0, 0.0, row)
        pad_ref[x, TOP + cells_y : TOP + cells_y + 1, inner] = jnp.where(here == 0, row, 0.0)

    def fill(x, carry):
        for shift in range(3):
            for z in range(blocks):
                value = pad_ref[
                    x,
                    TOP - 1 + shift : TOP - 1 + shift + cells_y,
                    z * out_lanes : z * out_lanes + in_lanes,
                ]
                high, low = split(value)
                high_ref[shift, z, x] = high
                low_ref[shift, z, x] = low
        return carry

    lax.fori_loop(0, cells_x + 2, fill, 0)

    acc_ref[...] = jnp.zeros(acc_ref.shape, F32)

    def multiply(i, carry):
        shift_x = i // 3
        shift_y = i % 3
        rows = blocks * cells_x * cells_y
        high = high_ref[shift_y, :, pl.ds(shift_x, cells_x)].reshape(rows, in_lanes)
        low = low_ref[shift_y, :, pl.ds(shift_x, cells_x)].reshape(rows, in_lanes)
        table_high = table_high_ref[i]
        acc_ref[...] += dot(high, table_high) + (
            dot(high, table_low_ref[i]) + dot(low, table_high)
        )
        return carry

    lax.fori_loop(0, 9, multiply, 0)
    for z in range(blocks):
        for x in range(cells_x):
            start = (z * cells_x + x) * cells_y
            value = acc_ref[start : start + cells_y, :]
            out_ref[x, :, z * out_lanes : (z + 1) * out_lanes] = gelu(value) if activate else value


def convolve(cells, weight, activate):
    cells_x, cells_y, width = cells.shape
    count = lax.axis_size("gx")
    before = lax.ppermute(cells[cells_x - 1 :], "gx", [(i, i + 1) for i in range(count - 1)])
    after = lax.ppermute(cells[:1], "gx", [(i + 1, i) for i in range(count - 1)])
    planes = (before, cells, after)
    first = jnp.concatenate([plane[:, 0] for plane in planes], axis=0)
    last = jnp.concatenate([plane[:, cells_y - 1] for plane in planes], axis=0)
    rim = lax.ppermute(
        jnp.where(lax.axis_index("gy") == 0, last, first), "gy", [(0, 1), (1, 0)]
    )
    blocks = NZ // BLOCK
    rows = blocks * cells_x * cells_y
    return pl.pallas_call(
        functools.partial(conv_kernel, activate=activate),
        out_shape=jax.ShapeDtypeStruct(cells.shape, F32),
        in_specs=[VMEM] * 5,
        out_specs=VMEM,
        scratch_shapes=[
            pltpu.VMEM((cells_x + 2, cells_y + 2 * TOP, width + 2 * LANES), F32),
            pltpu.VMEM((3, blocks, cells_x + 2, cells_y, WINDOW * CH), BF16),
            pltpu.VMEM((3, blocks, cells_x + 2, cells_y, WINDOW * CH), BF16),
            pltpu.VMEM((9, WINDOW * CH, BLOCK * CH), BF16),
            pltpu.VMEM((9, WINDOW * CH, BLOCK * CH), BF16),
            pltpu.VMEM((rows, BLOCK * CH), F32),
        ],
        compiler_params=pltpu.CompilerParams(vmem_limit_bytes=22 << 20),
        cost_estimate=pl.CostEstimate(
            flops=6 * rows * 9 * WINDOW * CH * BLOCK * CH, transcendentals=0, bytes_accessed=1 << 21
        ),
    )(cells, before, after, rim, weight.reshape(9, 3 * CH, CH))


def all_to_all(value):
    return lax.all_to_all(value, "gx", split_axis=0, concat_axis=0, tiled=True)


def block(field, spectral, conv_first, conv_second, bias):
    cells_x, cells_y, width = field.shape
    devices_x = lax.axis_size("gx")
    devices_y = lax.axis_size("gy")
    extent_x = cells_x * devices_x
    extent_y = cells_y * devices_y
    owned_y = MY // devices_y
    wide = MZ // GROUP
    pair = ROWS // (2 * cells_x)
    tiles = owned_y // pair * wide
    assert devices_y == 2 and tiles == devices_x and MX == devices_x

    forward_y = np.moveaxis(host_split(forward_tables(cells_x, cells_y, devices_y)), 0, 2)
    inverse_y = np.moveaxis(host_split(inverse_tables(cells_x, cells_y, devices_y)), 0, 2)
    forward_x, inverse_x = (host_split(t) for t in x_tables(cells_x, devices_x, pair))
    twiddle_out = z_twiddle(1)
    weights = np.where(np.arange(MZ) == 0, 1.0, 2.0) / (extent_x * extent_y * NZ)
    twiddle_out = (twiddle_out * weights[None, :, None]).astype(np.float32)

    tile_shape = jax.ShapeDtypeStruct((tiles, ROWS, LANES), F32)
    keep, send = pl.pallas_call(
        functools.partial(forward_kernel, devices_y=devices_y),
        out_shape=(tile_shape, tile_shape),
        in_specs=[VMEM] * 3,
        out_specs=(VMEM, VMEM),
        scratch_shapes=[pltpu.VMEM((2 * cells_x * cells_y, MZ * CH), F32)],
        compiler_params=small_grant(),
    )(field.reshape(cells_x * cells_y, width), forward_y, z_twiddle(-1))
    lines = keep + lax.ppermute(send, "gy", [(0, 1), (1, 0)])
    lines, cells, spectral = lax.optimization_barrier((lines, field, spectral))

    columns = all_to_all(lines)
    hidden = convolve(cells, conv_first, True)
    modes = apply_matrix(forward_x, columns.reshape(-1, LANES))
    modes = all_to_all(modes.reshape(MX, 2 * pair, LANES))

    count = tiles * pair
    halves = GROUP * count // LANES
    matrix = spectral.reshape(
        owned_y // pair, pair, wide, halves, GROUP // halves, 2, CH, CH
    ).transpose(5, 3, 6, 7, 4, 0, 2, 1)
    matrix = matrix.reshape(2, halves, CH, CH, LANES)
    mixed = pl.pallas_call(
        mix_kernel,
        out_shape=jax.ShapeDtypeStruct((2 * count, LANES), F32),
        in_specs=[VMEM, VMEM],
        out_specs=VMEM,
        compiler_params=small_grant(),
    )(modes.reshape(2 * count, LANES), matrix)
    columns = all_to_all(mixed.reshape(tiles, 2 * pair, LANES))
    branch = convolve(hidden, conv_second, False)
    lines = apply_matrix(inverse_x, columns.reshape(-1, LANES))
    own = all_to_all(lines.reshape(devices_x, ROWS, LANES))
    other = lax.ppermute(own, "gy", [(0, 1), (1, 0)])
    result = pl.pallas_call(
        functools.partial(end_kernel, devices_y=devices_y),
        out_shape=jax.ShapeDtypeStruct((cells_x * cells_y, width), F32),
        in_specs=[VMEM] * 6,
        out_specs=VMEM,
        scratch_shapes=[pltpu.VMEM((2 * cells_x * cells_y, MZ * CH), F32)],
        compiler_params=small_grant(),
    )(
        own, other, inverse_y, twiddle_out, branch.reshape(cells_x * cells_y, width),
        jnp.tile(bias, GROUP).reshape(1, LANES),
    )
    return result.reshape(cells_x, cells_y, width)


def solution(mesh):
    in_specs = (
        P(("groups", "gx"), "gy", None),
        P("gy", "gx", None, None, None, None),
        P(),
        P(),
        P(),
    )
    out_specs = P(("groups", "gx"), "gy", None)
    return jax.shard_map(block, mesh=mesh, in_specs=in_specs, out_specs=out_specs, check_vma=False)
```

time: 382 us -> 209 us (0.55); the launches traced: 375 us -> 208 us
  matrix products: 147 us -> 0 us
  local copies, waits for them, and re-layouts: 75.2 us -> 26.3 us
  waiting for transfers between devices: 31.8 us -> 69.4 us
  Pallas kernels: 0 us -> 24.2 us
  loops' own time: 15 us -> 0 us
  blocking collectives: 8.41 us -> 0 us
  starting transfers between devices: 91.8 us -> 86.8 us
  other arithmetic: 4.77 us -> 0.77 us
    dot_general x60 -> x0, matrix products: 147 us -> none  [the longest x36 112 us: plane(): jnp.einsum('yzi,io->yzo', stacked, kernel[shift_x, shift_y], precision=HI...]
    all_to_all x4, waiting for transfers between devices: 24.8 us -> 53.9 us  [all_to_all(): return lax.all_to_all(value, 'gx', split_axis=0, concat_axis=0, tiled=True)]
    pallas_call x0 -> x7, Pallas kernels: none -> 24.2 us  [the longest x2 16.7 us: convolve(): pl.pallas_call(functools.partial(conv_kernel, activate=activate), out_sha...]
    all_to_all x4, starting transfers between devices: 71.9 us -> 48.5 us  [all_to_all(): return lax.all_to_all(value, 'gx', split_axis=0, concat_axis=0, tiled=True)]
    squeeze x4 -> x6, local copies, waits for them, and re-layouts: 20.9 us -> 0.08 us  [convolve(): first = jnp.concatenate([plane[:, 0] for plane in planes], axis=0)]
    ppermute x8, starting transfers between devices: 19.9 us -> 38.3 us  [the longest x1 20.5 us: block(): lines = keep + lax.ppermute(send, 'gy', [(0, 1), (1, 0)])]
    slice x32 -> x3, local copies, waits for them, and re-layouts: 19 us -> 1.92 us  [the longest x2 1.9 us: convolve(): cells[:1]]
    another operation x2 -> x0, loops' own time: 15 us -> none  [convolve(): return lax.map(plane, jnp.arange(extent_x, dtype=jnp.int32))]
  transfers between devices with their start and end apart: 12 -> 12, of which waited for: 5 -> 5; matrix products, arithmetic and copies ran while one was open for 56% -> 8% of each run, Pallas kernels for 0% -> 9%
where the time goes in v1:
time: 209 us; the launch traced here: 208 us
  starting transfers between devices  86.8 us (42%)
  waiting for transfers between devices  69.4 us (33%)
  local copies, waits for them, and re-layouts  26.3 us (13%)
  Pallas kernels  24.2 us (12%)
    all_to_all x4, waiting for transfers between devices, all_to_all(): return lax.all_to_all(value, 'gx', split_axis=0, concat_axis=0, tiled=True)  53.9 us
    all_to_all x4, starting transfers between devices, all_to_all(): return lax.all_to_all(value, 'gx', split_axis=0, concat_axis=0, tiled=True)  48.5 us
    ppermute x1, starting transfers between devices, block(): lines = keep + lax.ppermute(send, 'gy', [(0, 1), (1, 0)])  20.5 us
    pallas_call x2, Pallas kernels, convolve(): pl.pallas_call(functools.partial(conv_kernel, activate=activate), out_sha...  16.7 us
    ppermute x2, waiting for transfers between devices, convolve(): lax.ppermute(cells[:1], 'gx', [(i + 1, i) for i in range(count - 1)])  14.5 us
    reshape x1, local copies, waits for them, and re-layouts, block(): spectral.reshape(owned_y // pair, pair, wide, halves, GROUP // halves, 2,...  8.12 us
    unnamed x30, local copies, waits for them, and re-layouts  8.03 us
    reshape x1, local copies, waits for them, and re-layouts, block(): matrix = matrix.reshape(2, halves, CH, CH, LANES)  6.6 us
  transfers between devices with their start and end apart: 12, of which 5 were waited for; matrix products, arithmetic and copies ran while one was open for 8% of the time, Pallas kernels for 9%

profile of v1, /device:TPU:37, one launch (start us, length us, event | category | flops | bytes accessed | tf_op | source)
XLA Modules:
  0.0 207.7 jit_solution(18276719619778949703)
XLA Ops:
  0.0 1.0 copy-done
  1.0 0.9 copy-done.5
  2.7 1.8 shard_map.109
  4.4 20.5 %collective-permute-start = (f32[32,8,128]{2,1,0:T(8,128)S(1)}, f32[32,8,128]{2,1,0:T(8,128)S(1)}, u32[]{:S(2)}, u32[]{:S(2)}) collective-permute-start(f32[32,8,128]{2,1,0:T(8,128)S(1)} %get-tuple-element.11), channel_id=1, source_target_pairs={{0,1},{1,0},{2,3},{3,2},{4,5},{5,4},{6,7},{7,6},{8,9},{9,8},{10,11... | collective-permute-start | bytes 393224 | tf_op jit(solution)/shard_map/ppermute | solution.py:465
  25.0 1.0 collective-permute-done
  26.6 1.1 fusion.2
  27.7 1.4 copy.19
  29.1 13.4 %all-to-all-start = ((f32[32,8,128]{2,1,0:T(8,128)}), f32[32,8,128]{2,1,0:T(8,128)S(1)}, u32[]{:S(2)}, u32[]{:S(2)}) async-start(f32[32,8,128]{2,1,0:T(8,128)} %add.3), calls=%async_computation | async-start | bytes 262144 | tf_op jit(solution)/shard_map/all_to_all | solution.py:434
  42.6 2.7 %collective-permute-start.2 = (f32[1,32,2048]{2,1,0:T(8,128)S(1)}, f32[1,32,2048]{2,1,0:T(8,128)S(1)}, u32[]{:S(2)}, u32[]{:S(2)}) collective-permute-start(f32[1,32,2048]{2,1,0:T(8,128)S(1)} %get-tuple-element.22), channel_id=1, source_target_pairs={{0,2},{2,4},{4,6},{6,8},{8,10},{10,12},{12,14},{14,16},{16,18},{18... | collective-permute-start | bytes 786440 | tf_op jit(solution)/shard_map/ppermute | solution.py:403
  45.3 1.3 collective-permute-start.3
  46.6 14.5 %collective-permute-done.3.after_ref = f32[1,32,2048]{2,1,0:T(8,128)S(1)} collective-permute-done((f32[1,32,2048]{2,1,0:T(8,128)S(1)}, f32[1,32,2048]{2,1,0:T(8,128)S(1)}, u32[]{:S(2)}, u32[]{:S(2)}) %collective-permute-start.3) | collective-permute-done | bytes 262176 | tf_op jit(solution)/shard_map/ppermute | solution.py:404
  62.6 0.9 collective-permute-start.4
  63.6 8.1 %copy.17 = f32[8,2,4,2,2,2,32,32]{7,6,1,2,0,4,3,5:T(8,128)} copy(f32[8,2,4,2,2,2,32,32]{7,6,5,4,3,2,1,0:T(8,128)} %bitcast.47) | data formatting | bytes 4194304 | tf_op jit(solution)/shard_map/reshape | solution.py:475
  71.7 6.6 %copy.18.weight_ref = f32[2,2,32,32,128]{4,3,2,1,0:T(8,128)S(1)} copy(f32[2,2,32,32,128]{3,2,4,1,0:T(8,128)} %bitcast.46) | data formatting | bytes 4194304 | tf_op jit(solution)/shard_map/reshape | solution.py:478
  79.2 20.7 %all-to-all-start.1 = ((f32[32,4,128]{2,1,0:T(4,128)}), f32[32,4,128]{2,1,0:T(4,128)S(1)}, u32[]{:S(2)}, u32[]{:S(2)}) async-start(f32[32,4,128]{2,1,0:T(4,128)} %bitcast.2), calls=%async_computation.1 | async-start | bytes 131072 | tf_op jit(solution)/shard_map/all_to_all | solution.py:434
  99.9 0.9 copy-done.9
  100.9 0.9 copy-done.11
  101.8 1.0 copy-done.12
  102.8 8.4 %shard_map.113.cells_ref = f32[2,32,2048]{2,1,0:T(8,128)S(1)} custom-call(f32[2,32,2048]{2,1,0:T(8,128)S(1)} %copy-done.1, f32[1,32,2048]{2,1,0:T(8,128)S(1)} %copy-done.9, f32[1,32,2048]{2,1,0:T(8,128)S(1)} %copy-done.11, f32[4,2048]{1,0:T(4,128)S(1)} %collective-permute-done.4.rim_ref, f32[9,96,32]{2,1,0:T(8,128)S(1)} %bitcast.44), custom_call_target="tpu_custom_call" | custom-call | flops 3623878656 | bytes 2097152 | tf_op jit(solution)/shard_map/pallas_call | solution.py:413
  112.1 12.1 %all-to-all-done.1 = f32[32,4,128]{2,1,0:T(4,128)S(1)} async-done(((f32[32,4,128]{2,1,0:T(4,128)}), f32[32,4,128]{2,1,0:T(4,128)S(1)}, u32[]{:S(2)}, u32[]{:S(2)}) %all-to-all-start.1) | async-done | bytes 65568 | tf_op jit(solution)/shard_map/all_to_all | solution.py:434
  124.2 1.3 shard_map.111
  125.5 9.3 %all-to-all-start.2 = ((f32[32,4,128]{2,1,0:T(4,128)}), f32[32,4,128]{2,1,0:T(4,128)S(1)}, u32[]{:S(2)}, u32[]{:S(2)}) async-start(f32[32,4,128]{2,1,0:T(4,128)} %bitcast.7), calls=%async_computation.2 | async-start | bytes 131072 | tf_op jit(solution)/shard_map/all_to_all | solution.py:434
  134.8 2.7 %collective-permute-start.5 = (f32[1,32,2048]{2,1,0:T(8,128)}, f32[1,32,2048]{2,1,0:T(8,128)S(1)}, u32[]{:S(2)}, u32[]{:S(2)}) collective-permute-start(f32[1,32,2048]{2,1,0:T(8,128)} %get-tuple-element.18), channel_id=1, source_target_pairs={{0,2},{2,4},{4,6},{6,8},{8,10},{10,12},{12,14},{14,16},{16,18},{18... | collective-permute-start | bytes 786440 | tf_op jit(solution)/shard_map/ppermute | solution.py:403
  137.6 1.3 collective-permute-start.6
  138.9 19.0 %all-to-all-done.2 = f32[32,4,128]{2,1,0:T(4,128)S(1)} async-done(((f32[32,4,128]{2,1,0:T(4,128)}), f32[32,4,128]{2,1,0:T(4,128)S(1)}, u32[]{:S(2)}, u32[]{:S(2)}) %all-to-all-start.2) | async-done | bytes 65568 | tf_op jit(solution)/shard_map/all_to_all | solution.py:434
  158.8 5.0 %all-to-all-start.3 = ((f32[32,8,128]{2,1,0:T(8,128)}), f32[32,8,128]{2,1,0:T(8,128)S(1)}, u32[]{:S(2)}, u32[]{:S(2)}) async-start(f32[32,8,128]{2,1,0:T(8,128)} %bitcast.9), calls=%async_computation.3 | async-start | bytes 262144 | tf_op jit(solution)/shard_map/all_to_all | solution.py:434
  163.9 3.2 %collective-permute-start.7 = (f32[4,2048]{1,0:T(4,128)S(1)}, f32[4,2048]{1,0:T(4,128)S(1)}, u32[]{:S(2)}, u32[]{:S(2)}) collective-permute-start(f32[4,2048]{1,0:T(4,128)S(1)} %maximum_select_fusion.1), channel_id=1, source_target_pairs={{0,1},{1,0},{2,3},{3,2},{4,5},{5,4},{6,7},{7,6},{8,9},{9,8},{10,11... | collective-permute-start | bytes 98312 | tf_op jit(solution)/shard_map/ppermute | solution.py:408
  167.2 22.8 %all-to-all-done.3.own_ref = f32[32,8,128]{2,1,0:T(8,128)S(1)} async-done(((f32[32,8,128]{2,1,0:T(8,128)}), f32[32,8,128]{2,1,0:T(8,128)S(1)}, u32[]{:S(2)}, u32[]{:S(2)}) %all-to-all-start.3) | async-done | bytes 131104 | tf_op jit(solution)/shard_map/all_to_all | solution.py:434
  190.0 5.5 %collective-permute-start.1 = (f32[32,8,128]{2,1,0:T(8,128)S(1)}, f32[32,8,128]{2,1,0:T(8,128)S(1)}, u32[]{:S(2)}, u32[]{:S(2)}) collective-permute-start(f32[32,8,128]{2,1,0:T(8,128)S(1)} %all-to-all-done.3.own_ref), channel_id=1, source_target_pairs={{0,1},{1,0},{2,3},{3,2},{4,5},{5,4},{6,7},{7,6},{8,9},{9,8},{10,11... | collective-permute-start | bytes 393224 | tf_op jit(solution)/shard_map/ppermute | solution.py:490
  195.5 1.0 copy-done.13
  196.5 8.3 %shard_map.114 = f32[2,32,2048]{2,1,0:T(8,128)S(1)} custom-call(f32[2,32,2048]{2,1,0:T(8,128)S(1)} %shard_map.113.cells_ref, f32[1,32,2048]{2,1,0:T(8,128)S(1)} %collective-permute-done.5.before_ref, f32[1,32,2048]{2,1,0:T(8,128)S(1)} %collective-permute-done.6.after_ref, f32[4,2048]{1,0:T(4,128)S(1)} %collective-permute-done.7.rim_ref, ...), custom_call_target="tpu_custom_call" | custom-call | flops 3623878656 | bytes 2097152 | tf_op jit(solution)/shard_map/pallas_call | solution.py:413
  204.9 2.8 %shard_map.115 = f32[64,2048]{1,0:T(8,128)} custom-call(f32[32,8,128]{2,1,0:T(8,128)S(1)} %all-to-all-done.3.own_ref, f32[32,8,128]{2,1,0:T(8,128)S(1)} %collective-permute-done.1.other_ref, bf16[2,2,2,128,64]{4,3,2,1,0:T(8,128)(2,1)S(1)} %copy-done.2, f32[2,16,128]{2,1,0:T(8,128)S(1)} %copy-done.6, f32[64,2048]{1,0:T(8,128)S(1)} %bitcast.40, ...), custom_call_target="tpu_custom_call" | custom-call | tf_op jit(solution)/shard_map/pallas_call | solution.py:491
  (46 shorter events, 5.7 us)
Async XLA Ops:
  0.0 1.0 copy-start
  1.0 0.9 copy-start.5
  1.9 0.7 copy-start.7
  4.4 21.5 %collective-permute-start = (f32[32,8,128]{2,1,0:T(8,128)S(1)}, f32[32,8,128]{2,1,0:T(8,128)S(1)}, u32[]{:S(2)}, u32[]{:S(2)}) collective-permute-start(f32[32,8,128]{2,1,0:T(8,128)S(1)} %get-tuple-element.11), channel_id=1, source_target_pairs={{0,1},{1,0},{2,3},{3,2},{4,5},{5,4},{6,7},{7,6},{8,9},{9,8},{10,11... | collective-permute-start | bytes 393224 | tf_op jit(solution)/shard_map/ppermute | solution.py:465
  29.1 49.2 %all-to-all-start = ((f32[32,8,128]{2,1,0:T(8,128)}), f32[32,8,128]{2,1,0:T(8,128)S(1)}, u32[]{:S(2)}, u32[]{:S(2)}) async-start(f32[32,8,128]{2,1,0:T(8,128)} %add.3), calls=%async_computation | async-start | bytes 262144 | tf_op jit(solution)/shard_map/all_to_all | solution.py:434
  42.6 19.3 %collective-permute-start.2 = (f32[1,32,2048]{2,1,0:T(8,128)S(1)}, f32[1,32,2048]{2,1,0:T(8,128)S(1)}, u32[]{:S(2)}, u32[]{:S(2)}) collective-permute-start(f32[1,32,2048]{2,1,0:T(8,128)S(1)} %get-tuple-element.22), channel_id=1, source_target_pairs={{0,2},{2,4},{4,6},{6,8},{8,10},{10,12},{12,14},{14,16},{16,18},{18... | collective-permute-start | bytes 786440 | tf_op jit(solution)/shard_map/ppermute | solution.py:403
  45.3 15.8 %collective-permute-start.3 = (f32[1,32,2048]{2,1,0:T(8,128)S(1)}, f32[1,32,2048]{2,1,0:T(8,128)S(1)}, u32[]{:S(2)}, u32[]{:S(2)}) collective-permute-start(f32[1,32,2048]{2,1,0:T(8,128)S(1)} %get-tuple-element.21), channel_id=1, source_target_pairs={{2,0},{4,2},{6,4},{8,6},{10,8},{12,10},{14,12},{16,14},{18,16},{20... | collective-permute-start | bytes 786440 | tf_op jit(solution)/shard_map/ppermute | solution.py:404
  61.1 0.7 copy-start.10
  61.9 0.7 copy-start.8
  62.6 37.3 %collective-permute-start.4 = (f32[4,2048]{1,0:T(4,128)S(1)}, f32[4,2048]{1,0:T(4,128)S(1)}, u32[]{:S(2)}, u32[]{:S(2)}) collective-permute-start(f32[4,2048]{1,0:T(4,128)S(1)} %maximum_select_fusion), channel_id=1, source_target_pairs={{0,1},{1,0},{2,3},{3,2},{4,5},{5,4},{6,7},{7,6},{8,9},{9,8},{10,11... | collective-permute-start | bytes 98312 | tf_op jit(solution)/shard_map/ppermute | solution.py:408
  71.7 6.6 %copy-start.4 = (bf16[2,128,256]{2,1,0:T(8,128)(2,1)S(1)}, bf16[2,128,256]{2,1,0:T(8,128)(2,1)}, u32[]{:S(2)}) copy-start(bf16[2,128,256]{2,1,0:T(8,128)(2,1)} %constant.20.clone.table_ref) | copy-start | bytes 393220
  71.7 28.2 %copy-start.1 = (f32[2,32,2048]{2,1,0:T(8,128)S(1)}, f32[2,32,2048]{2,1,0:T(8,128)}, u32[]{:S(2)}) copy-start(f32[2,32,2048]{2,1,0:T(8,128)} %cells_ref) | copy-start | bytes 1572868
  79.2 45.1 %all-to-all-start.1 = ((f32[32,4,128]{2,1,0:T(4,128)}), f32[32,4,128]{2,1,0:T(4,128)S(1)}, u32[]{:S(2)}, u32[]{:S(2)}) async-start(f32[32,4,128]{2,1,0:T(4,128)} %bitcast.2), calls=%async_computation.1 | async-start | bytes 131072 | tf_op jit(solution)/shard_map/all_to_all | solution.py:434
  99.9 1.0 copy-start.9
  100.9 0.9 copy-start.11
  101.8 1.0 copy-start.12
  102.8 55.1 %copy-start.3 = (bf16[2,256,128]{2,1,0:T(8,128)(2,1)S(1)}, bf16[2,256,128]{2,1,0:T(8,128)(2,1)}, u32[]{:S(2)}) copy-start(bf16[2,256,128]{2,1,0:T(8,128)(2,1)} %constant.21.clone.table_ref) | copy-start | bytes 393220
  102.8 64.3 %copy-start.14 = (f32[32]{0:T(128)S(1)}, f32[32]{0:T(128)}, u32[]{:S(2)}) copy-start(f32[32]{0:T(128)} %param.15) | copy-start | bytes 388
  112.1 92.8 %copy-start.2 = (bf16[2,2,2,128,64]{4,3,2,1,0:T(8,128)(2,1)S(1)}, bf16[2,2,2,128,64]{4,3,2,1,0:T(8,128)(2,1)}, u32[]{:S(2)}) copy-start(bf16[2,2,2,128,64]{4,3,2,1,0:T(8,128)(2,1)} %constant.22.clone.table_ref) | copy-start | bytes 393220
  112.1 92.8 %copy-start.6 = (f32[2,16,128]{2,1,0:T(8,128)S(1)}, f32[2,16,128]{2,1,0:T(8,128)}, u32[]{:S(2)}) copy-start(f32[2,16,128]{2,1,0:T(8,128)} %constant.23.clone.twiddle_ref) | copy-start | bytes 49156
  125.5 32.4 %all-to-all-start.2 = ((f32[32,4,128]{2,1,0:T(4,128)}), f32[32,4,128]{2,1,0:T(4,128)S(1)}, u32[]{:S(2)}, u32[]{:S(2)}) async-start(f32[32,4,128]{2,1,0:T(4,128)} %bitcast.7), calls=%async_computation.2 | async-start | bytes 131072 | tf_op jit(solution)/shard_map/all_to_all | solution.py:434
  134.8 29.0 %collective-permute-start.5 = (f32[1,32,2048]{2,1,0:T(8,128)}, f32[1,32,2048]{2,1,0:T(8,128)S(1)}, u32[]{:S(2)}, u32[]{:S(2)}) collective-permute-start(f32[1,32,2048]{2,1,0:T(8,128)} %get-tuple-element.18), channel_id=1, source_target_pairs={{0,2},{2,4},{4,6},{6,8},{8,10},{10,12},{12,14},{14,16},{16,18},{18... | collective-permute-start | bytes 786440 | tf_op jit(solution)/shard_map/ppermute | solution.py:403
  137.6 26.2 %collective-permute-start.6 = (f32[1,32,2048]{2,1,0:T(8,128)}, f32[1,32,2048]{2,1,0:T(8,128)S(1)}, u32[]{:S(2)}, u32[]{:S(2)}) collective-permute-start(f32[1,32,2048]{2,1,0:T(8,128)} %get-tuple-element.17), channel_id=1, source_target_pairs={{2,0},{4,2},{6,4},{8,6},{10,8},{12,10},{14,12},{16,14},{18,16},{20... | collective-permute-start | bytes 786440 | tf_op jit(solution)/shard_map/ppermute | solution.py:404
  158.8 31.2 %all-to-all-start.3 = ((f32[32,8,128]{2,1,0:T(8,128)}), f32[32,8,128]{2,1,0:T(8,128)S(1)}, u32[]{:S(2)}, u32[]{:S(2)}) async-start(f32[32,8,128]{2,1,0:T(8,128)} %bitcast.9), calls=%async_computation.3 | async-start | bytes 262144 | tf_op jit(solution)/shard_map/all_to_all | solution.py:434
  163.9 31.6 %collective-permute-start.7 = (f32[4,2048]{1,0:T(4,128)S(1)}, f32[4,2048]{1,0:T(4,128)S(1)}, u32[]{:S(2)}, u32[]{:S(2)}) collective-permute-start(f32[4,2048]{1,0:T(4,128)S(1)} %maximum_select_fusion.1), channel_id=1, source_target_pairs={{0,1},{1,0},{2,3},{3,2},{4,5},{5,4},{6,7},{7,6},{8,9},{9,8},{10,11... | collective-permute-start | bytes 98312 | tf_op jit(solution)/shard_map/ppermute | solution.py:408
  190.0 14.9 %collective-permute-start.1 = (f32[32,8,128]{2,1,0:T(8,128)S(1)}, f32[32,8,128]{2,1,0:T(8,128)S(1)}, u32[]{:S(2)}, u32[]{:S(2)}) collective-permute-start(f32[32,8,128]{2,1,0:T(8,128)S(1)} %all-to-all-done.3.own_ref), channel_id=1, source_target_pairs={{0,1},{1,0},{2,3},{3,2},{4,5},{5,4},{6,7},{7,6},{8,9},{9,8},{10,11... | collective-permute-start | bytes 393224 | tf_op jit(solution)/shard_map/ppermute | solution.py:490
  195.5 1.0 copy-start.13

commit v2 on v1

--- a/solution.py
+++ b/solution.py
@@ -126,9 +126,30 @@
     return out
 
 
-def forward_kernel(cells_ref, table_ref, twiddle_ref, keep_ref, send_ref, z_ref, *, devices_y):
+def forward_kernel(
+    cells_hbm, table_hbm, twiddle_hbm, keep_ref, send_ref, z_ref, cells_ref, table_ref,
+    twiddle_ref, sems, *, devices_y,
+):
     rows = cells_ref.shape[0]
+    here = lax.axis_index("gy")
+    there = devices_y - 1 - here
     lane = lax.broadcasted_iota(jnp.int32, (ROWS, LANES), 1)
+    half_rows = rows // 2
+    twiddle_copy = pltpu.make_async_copy(twiddle_hbm, twiddle_ref, sems.at[0])
+    table_copy = pltpu.make_async_copy(table_hbm.at[here], table_ref, sems.at[1])
+    cell_copies = [
+        pltpu.make_async_copy(
+            cells_hbm.at[pl.ds(part * half_rows, half_rows)],
+            cells_ref.at[pl.ds(part * half_rows, half_rows)],
+            sems.at[2 + part],
+        )
+        for part in range(2)
+    ]
+    twiddle_copy.start()
+    cell_copies[0].start()
+    cell_copies[1].start()
+    table_copy.start()
+    twiddle_copy.wait()
 
     def step(i, carry):
         start = pl.multiple_of(i * ROWS, ROWS)
@@ -146,16 +167,18 @@
             z_ref[pl.ds(start + rows, ROWS), h * LANES : (h + 1) * LANES] = imag[h]
         return carry
 
-    lax.fori_loop(0, rows // ROWS, step, 0)
-    here = lax.axis_index("gy")
-    there = devices_y - 1 - here
+    steps = half_rows // ROWS
+    for part in range(2):
+        cell_copies[part].wait()
+        lax.fori_loop(part * steps, (part + 1) * steps, step, 0)
+    table_copy.wait()
     high, low = split(z_ref[...])
     for target, out_ref in ((there, send_ref), (here, keep_ref)):
-        table = table_ref[here, target, 0]
-        modes = dot(table, high) + (dot(table_ref[here, target, 1], high) + dot(table, low))
+        table = table_ref[target, 0]
+        modes = dot(table, high) + (dot(table_ref[target, 1], high) + dot(table, low))
         for h in range(MZ // GROUP):
             for kp in range(modes.shape[0] // ROWS):
-                out_ref[kp * (MZ // GROUP) + h] = modes[
+                out_ref[h * (modes.shape[0] // ROWS) + kp] = modes[
                     kp * ROWS : (kp + 1) * ROWS, h * LANES : (h + 1) * LANES
                 ]
 
@@ -190,6 +213,27 @@
         out_specs=VMEM,
         compiler_params=small_grant(),
     )(table, value)
+
+
+def arrange_kernel(weight_ref, out_ref, *, owned_y):
+    halves, channels = out_ref.shape[1:3]
+    wide = MZ // GROUP
+    per = GROUP // halves
+    stride = MZ * 2 * channels
+
+    def step(c, carry):
+        for part in range(2):
+            for h in range(halves):
+                pieces = []
+                for g in range(per):
+                    for block in range(wide):
+                        kz = block * GROUP + h * per + g
+                        first = (kz * 2 + part) * channels + c
+                        pieces.append(weight_ref[pl.ds(first, owned_y, stride=stride), :])
+                out_ref[part, h, c] = jnp.concatenate(pieces, axis=0).T
+        return carry
+
+    lax.fori_loop(0, channels, step, 0)
 
 
 def mix_kernel(modes_ref, weight_ref, out_ref):
@@ -254,7 +298,7 @@
         pairs = ref.shape[0] // wide
         return jnp.concatenate(
             [
-                jnp.concatenate([ref[kp * wide + h] for kp in range(pairs)], axis=0)
+                jnp.concatenate([ref[h * pairs + kp] for kp in range(pairs)], axis=0)
                 for h in range(wide)
             ],
             axis=1,
@@ -317,9 +361,10 @@
 
 
 def conv_kernel(
-    cells_ref, before_ref, after_ref, rim_ref, weight_ref, out_ref, pad_ref, high_ref, low_ref,
-    table_high_ref, table_low_ref, acc_ref, *, activate,
+    first_ref, second_ref, rim_ref, weight_ref, out_ref, pad_ref, high_ref, low_ref,
+    table_high_ref, table_low_ref, acc_ref, *, shifted, activate,
 ):
+    cells_ref = first_ref
     cells_x, cells_y, width = cells_ref.shape
     here = lax.axis_index("gy")
     blocks = NZ // BLOCK
@@ -341,26 +386,35 @@
                 for e in range(3):
                     place = z - (GROUP - 1) - e
                     if 0 <= place < BLOCK:
-                        term = jnp.where(group == place, wide[e * CH : (e + 1) * CH], 0.0)
-                        total = term if total is None else total + term
+                        other = 0.0 if total is None else total
+                        total = jnp.where(group == place, wide[e * CH : (e + 1) * CH], other)
                 ref[i, z * CH : (z + 1) * CH, :] = zero if total is None else total.astype(BF16)
         return carry
 
     lax.fori_loop(0, 9, build, 0)
 
-    pad_ref[:, :, :LANES] = jnp.zeros((cells_x + 2, pad_ref.shape[1], LANES), F32)
-    pad_ref[:, :, LANES + width :] = jnp.zeros((cells_x + 2, pad_ref.shape[1], LANES), F32)
+    pad_ref[:, :, :LANES] = jnp.zeros((2 * cells_x, pad_ref.shape[1], LANES), F32)
+    pad_ref[:, :, LANES + width :] = jnp.zeros((2 * cells_x, pad_ref.shape[1], LANES), F32)
     inner = slice(LANES, LANES + width)
-    pad_ref[0, TOP : TOP + cells_y, inner] = before_ref[0]
     for x in range(cells_x):
-        pad_ref[1 + x, TOP : TOP + cells_y, inner] = cells_ref[x]
-    pad_ref[1 + cells_x, TOP : TOP + cells_y, inner] = after_ref[0]
-    for x in range(cells_x + 2):
+        pad_ref[x, TOP : TOP + cells_y, inner] = first_ref[x]
+        pad_ref[cells_x + x, TOP : TOP + cells_y, inner] = second_ref[x]
+    for x in range(2 * cells_x):
         row = rim_ref[x : x + 1, :]
         pad_ref[x, TOP - 1 : TOP, inner] = jnp.where(here == 0, 0.0, row)
         pad_ref[x, TOP + cells_y : TOP + cells_y + 1, inner] = jnp.where(here == 0, row, 0.0)
 
-    def fill(x, carry):
+    place = lax.axis_index("gx")
+    at_start = place == 0
+    at_end = place == lax.axis_size("gx") - 1
+
+    def fill(slot, carry):
+        x = (slot + 1) // 2
+        if shifted:
+            outside = at_end & ((slot == 1) | (slot == 4))
+        else:
+            outside = (at_start & (slot == 0)) | (at_end & (slot == 5))
+        inside = jnp.where(outside, 0.0, 1.0)
         for shift in range(3):
             for z in range(blocks):
                 value = pad_ref[
@@ -368,12 +422,12 @@
                     TOP - 1 + shift : TOP - 1 + shift + cells_y,
                     z * out_lanes : z * out_lanes + in_lanes,
                 ]
-                high, low = split(value)
-                high_ref[shift, z, x] = high
-                low_ref[shift, z, x] = low
+                high, low = split(value * inside)
+                high_ref[shift, z, slot] = high
+                low_ref[shift, z, slot] = low
         return carry
 
-    lax.fori_loop(0, cells_x + 2, fill, 0)
+    lax.fori_loop(0, 3 * cells_x, fill, 0)
 
     acc_ref[...] = jnp.zeros(acc_ref.shape, F32)
 
@@ -381,8 +435,8 @@
         shift_x = i // 3
         shift_y = i % 3
         rows = blocks * cells_x * cells_y
-        high = high_ref[shift_y, :, pl.ds(shift_x, cells_x)].reshape(rows, in_lanes)
-        low = low_ref[shift_y, :, pl.ds(shift_x, cells_x)].reshape(rows, in_lanes)
+        high = high_ref[shift_y, :, pl.ds(shift_x * cells_x, cells_x)].reshape(rows, in_lanes)
+        low = low_ref[shift_y, :, pl.ds(shift_x * cells_x, cells_x)].reshape(rows, in_lanes)
         table_high = table_high_ref[i]
         acc_ref[...] += dot(high, table_high) + (
             dot(high, table_low_ref[i]) + dot(low, table_high)
@@ -397,37 +451,52 @@
             out_ref[x, :, z * out_lanes : (z + 1) * out_lanes] = gelu(value) if activate else value
 
 
-def convolve(cells, weight, activate):
-    cells_x, cells_y, width = cells.shape
-    count = lax.axis_size("gx")
-    before = lax.ppermute(cells[cells_x - 1 :], "gx", [(i, i + 1) for i in range(count - 1)])
-    after = lax.ppermute(cells[:1], "gx", [(i + 1, i) for i in range(count - 1)])
-    planes = (before, cells, after)
-    first = jnp.concatenate([plane[:, 0] for plane in planes], axis=0)
-    last = jnp.concatenate([plane[:, cells_y - 1] for plane in planes], axis=0)
-    rim = lax.ppermute(
-        jnp.where(lax.axis_index("gy") == 0, last, first), "gy", [(0, 1), (1, 0)]
-    )
+def rim_kernel(first_top, first_end, second_top, second_end, out_ref):
+    here = lax.axis_index("gy")
+    for i, (top, end) in enumerate(((first_top, first_end), (second_top, second_end))):
+        for x in range(top.shape[0]):
+            row = jnp.where(here == 0, end[x, ROWS - 1 : ROWS, :], top[x, 0:1, :])
+            out_ref[i * top.shape[0] + x : i * top.shape[0] + x + 1, :] = row
+
+
+def convolve(first, second, weight, shifted, activate):
+    cells_x, cells_y, width = first.shape
+    top = pl.BlockSpec((cells_x, ROWS, width), lambda i: (0, 0, 0))
+    end = pl.BlockSpec((cells_x, ROWS, width), lambda i: (0, cells_y // ROWS - 1, 0))
+    rim = pl.pallas_call(
+        rim_kernel,
+        grid=(1,),
+        out_shape=jax.ShapeDtypeStruct((2 * cells_x, width), F32),
+        in_specs=[top, end, top, end],
+        out_specs=pl.BlockSpec((2 * cells_x, width), lambda i: (0, 0)),
+        compiler_params=small_grant(),
+    )(first, first, second, second)
+    rim = lax.ppermute(rim, "gy", [(0, 1), (1, 0)])
+    return band_product(first, second, rim, weight, shifted, activate)
+
+
+def band_product(first, second, rim, weight, shifted, activate):
+    cells_x, cells_y, width = first.shape
     blocks = NZ // BLOCK
     rows = blocks * cells_x * cells_y
     return pl.pallas_call(
-        functools.partial(conv_kernel, activate=activate),
-        out_shape=jax.ShapeDtypeStruct(cells.shape, F32),
-        in_specs=[VMEM] * 5,
+        functools.partial(conv_kernel, shifted=shifted, activate=activate),
+        out_shape=jax.ShapeDtypeStruct(first.shape, F32),
+        in_specs=[VMEM] * 4,
         out_specs=VMEM,
         scratch_shapes=[
-            pltpu.VMEM((cells_x + 2, cells_y + 2 * TOP, width + 2 * LANES), F32),
-            pltpu.VMEM((3, blocks, cells_x + 2, cells_y, WINDOW * CH), BF16),
-            pltpu.VMEM((3, blocks, cells_x + 2, cells_y, WINDOW * CH), BF16),
+            pltpu.VMEM((2 * cells_x, cells_y + 2 * TOP, width + 2 * LANES), F32),
+            pltpu.VMEM((3, blocks, 3 * cells_x, cells_y, WINDOW * CH), BF16),
+            pltpu.VMEM((3, blocks, 3 * cells_x, cells_y, WINDOW * CH), BF16),
             pltpu.VMEM((9, WINDOW * CH, BLOCK * CH), BF16),
             pltpu.VMEM((9, WINDOW * CH, BLOCK * CH), BF16),
             pltpu.VMEM((rows, BLOCK * CH), F32),
         ],
-        compiler_params=pltpu.CompilerParams(vmem_limit_bytes=22 << 20),
+        compiler_params=pltpu.CompilerParams(vmem_limit_bytes=20 << 20),
         cost_estimate=pl.CostEstimate(
             flops=6 * rows * 9 * WINDOW * CH * BLOCK * CH, transcendentals=0, bytes_accessed=1 << 21
         ),
-    )(cells, before, after, rim, weight.reshape(9, 3 * CH, CH))
+    )(first, second, rim, weight.reshape(9, 3 * CH, CH))
 
 
 def all_to_all(value):
@@ -444,7 +513,7 @@
     wide = MZ // GROUP
     pair = ROWS // (2 * cells_x)
     tiles = owned_y // pair * wide
-    assert devices_y == 2 and tiles == devices_x and MX == devices_x
+    assert devices_y == 2 and cells_x == 2 and tiles == devices_x and MX == devices_x
 
     forward_y = np.moveaxis(host_split(forward_tables(cells_x, cells_y, devices_y)), 0, 2)
     inverse_y = np.moveaxis(host_split(inverse_tables(cells_x, cells_y, devices_y)), 0, 2)
@@ -457,25 +526,38 @@
     keep, send = pl.pallas_call(
         functools.partial(forward_kernel, devices_y=devices_y),
         out_shape=(tile_shape, tile_shape),
-        in_specs=[VMEM] * 3,
+        in_specs=[pl.BlockSpec(memory_space=pltpu.HBM)] * 3,
         out_specs=(VMEM, VMEM),
-        scratch_shapes=[pltpu.VMEM((2 * cells_x * cells_y, MZ * CH), F32)],
-        compiler_params=small_grant(),
+        scratch_shapes=[
+            pltpu.VMEM((2 * cells_x * cells_y, MZ * CH), F32),
+            pltpu.VMEM((cells_x * cells_y, width), F32),
+            pltpu.VMEM(forward_y.shape[1:], BF16),
+            pltpu.VMEM((2, MZ, LANES), F32),
+            pltpu.SemaphoreType.DMA((4,)),
+        ],
+        compiler_params=pltpu.CompilerParams(vmem_limit_bytes=58 << 20),
     )(field.reshape(cells_x * cells_y, width), forward_y, z_twiddle(-1))
     lines = keep + lax.ppermute(send, "gy", [(0, 1), (1, 0)])
     lines, cells, spectral = lax.optimization_barrier((lines, field, spectral))
 
     columns = all_to_all(lines)
-    hidden = convolve(cells, conv_first, True)
+    following = lax.ppermute(
+        cells, "gx", [((i + 1) % devices_x, i) for i in range(devices_x)]
+    )
+    hidden = convolve(cells, following, conv_first, True, True)
     modes = apply_matrix(forward_x, columns.reshape(-1, LANES))
     modes = all_to_all(modes.reshape(MX, 2 * pair, LANES))
 
     count = tiles * pair
     halves = GROUP * count // LANES
-    matrix = spectral.reshape(
-        owned_y // pair, pair, wide, halves, GROUP // halves, 2, CH, CH
-    ).transpose(5, 3, 6, 7, 4, 0, 2, 1)
-    matrix = matrix.reshape(2, halves, CH, CH, LANES)
+    matrix = pl.pallas_call(
+        functools.partial(arrange_kernel, owned_y=owned_y),
+        out_shape=jax.ShapeDtypeStruct((2, halves, CH, CH, LANES), F32),
+        in_specs=[VMEM],
+        out_specs=VMEM,
+        compiler_params=pltpu.CompilerParams(vmem_limit_bytes=24 << 20),
+        cost_estimate=pl.CostEstimate(flops=1 << 30, transcendentals=0, bytes_accessed=10 << 20),
+    )(spectral.reshape(-1, CH))
     mixed = pl.pallas_call(
         mix_kernel,
         out_shape=jax.ShapeDtypeStruct((2 * count, LANES), F32),
@@ -484,7 +566,10 @@
         compiler_params=small_grant(),
     )(modes.reshape(2 * count, LANES), matrix)
     columns = all_to_all(mixed.reshape(tiles, 2 * pair, LANES))
-    branch = convolve(hidden, conv_second, False)
+    previous = lax.ppermute(
+        hidden, "gx", [(i, (i + 1) % devices_x) for i in range(devices_x)]
+    )
+    branch = convolve(previous, hidden, conv_second, False, False)
     lines = apply_matrix(inverse_x, columns.reshape(-1, LANES))
     own = all_to_all(lines.reshape(devices_x, ROWS, LANES))
     other = lax.ppermute(own, "gy", [(0, 1), (1, 0)])

time: 209 us -> 184 us (0.88)
  blocking collectives: 0 us -> 42.4 us
  starting transfers between devices: 86.8 us -> 51.1 us
  waiting for transfers between devices: 69.4 us -> 47.5 us
  local copies, waits for them, and re-layouts: 26.3 us -> 4.41 us
  Pallas kernels: 24.2 us -> 37.2 us
    all_to_all x0 -> x1, blocking collectives: none -> 42.4 us  [all_to_all(): return lax.all_to_all(value, 'gx', split_axis=0, concat_axis=0, tiled=True)]
    all_to_all x4 -> x3, starting transfers between devices: 48.5 us -> 21.8 us  [all_to_all(): return lax.all_to_all(value, 'gx', split_axis=0, concat_axis=0, tiled=True)]
    all_to_all x4 -> x3, waiting for transfers between devices: 53.9 us -> 29.5 us  [all_to_all(): return lax.all_to_all(value, 'gx', split_axis=0, concat_axis=0, tiled=True)]
    reshape x2 -> x0, local copies, waits for them, and re-layouts: 14.7 us -> none  [the longest x1 8.12 us: block(): spectral.reshape(owned_y // pair, pair, wide, halves, GROUP // halves, 2,...]
    pallas_call x2 -> x5, Pallas kernels: 16.7 us -> 28 us  [the longest x2 17.9 us: band_product(): pl.pallas_call(functools.partial(conv_kernel, shifted=shifted, activate=a...]
    ppermute x1, starting transfers between devices: 5.51 us -> 0.18 us  [block(): other = lax.ppermute(own, 'gy', [(0, 1), (1, 0)])]
    unnamed x30 -> x18, local copies, waits for them, and re-layouts: 8.03 us -> 4.32 us
    ppermute x6 -> x4, starting transfers between devices: 12.2 us -> 8.61 us  [the longest x2 5.43 us: convolve(): rim = lax.ppermute(rim, 'gy', [(0, 1), (1, 0)])]
  transfers between devices with their start and end apart: 12 -> 9, of which waited for: 5 -> 6; matrix products, arithmetic and copies ran while one was open for 8% -> 0% of each run, Pallas kernels for 9% -> 16%
where the time goes in v2:
time: 184 us
  starting transfers between devices  51.1 us (28%)
  waiting for transfers between devices  47.5 us (26%)
  blocking collectives  42.4 us (23%)
  Pallas kernels  37.2 us (20%)
  local copies, waits for them, and re-layouts  4.41 us (2%)
    all_to_all x1, blocking collectives, all_to_all(): return lax.all_to_all(value, 'gx', split_axis=0, concat_axis=0, tiled=True)  42.4 us
    all_to_all x3, waiting for transfers between devices, all_to_all(): return lax.all_to_all(value, 'gx', split_axis=0, concat_axis=0, tiled=True)  29.5 us
    all_to_all x3, starting transfers between devices, all_to_all(): return lax.all_to_all(value, 'gx', split_axis=0, concat_axis=0, tiled=True)  21.8 us
    ppermute x1, starting transfers between devices, block(): lines = keep + lax.ppermute(send, 'gy', [(0, 1), (1, 0)])  20.5 us
    pallas_call x2, Pallas kernels, band_product(): pl.pallas_call(functools.partial(conv_kernel, shifted=shifted, activate=a...  17.9 us
    ppermute x1, waiting for transfers between devices, block(): lax.ppermute(hidden, 'gx', [(i, (i + 1) % devices_x) for i in range(devic...  15.3 us
    pallas_call x1, Pallas kernels, block(): pl.pallas_call(functools.partial(arrange_kernel, owned_y=owned_y), out_sh...  10.1 us
    ppermute x2, starting transfers between devices, convolve(): rim = lax.ppermute(rim, 'gy', [(0, 1), (1, 0)])  5.43 us
  transfers between devices with their start and end apart: 9, of which 6 were waited for; matrix products, arithmetic and copies ran while one was open for 0% of the time, Pallas kernels for 16%

profile of v2, /device:TPU:37, one launch (start us, length us, event | category | flops | bytes accessed | tf_op | source)
XLA Modules:
  0.0 183.8 jit_solution(7854880141770023812)
XLA Ops:
  0.0 3.5 %shard_map.109 = (f32[32,8,128]{2,1,0:T(8,128)}, f32[32,8,128]{2,1,0:T(8,128)}) custom-call(f32[64,2048]{1,0:T(8,128)} %bitcast.13, bf16[2,2,2,64,128]{4,3,2,1,0:T(8,128)(2,1)} %constant.12.clone.table_hbm, f32[2,16,128]{2,1,0:T(8,128)} %constant.13.clone.twiddle_hbm), custom_call_target="tpu_custom_call" | custom-call | tf_op jit(solution)/shard_map/pallas_call | solution.py:526
  3.5 0.0 copy-start.6
  3.5 20.5 %collective-permute-start = (f32[32,8,128]{2,1,0:T(8,128)}, f32[32,8,128]{2,1,0:T(8,128)S(1)}, u32[]{:S(2)}, u32[]{:S(2)}) collective-permute-start(f32[32,8,128]{2,1,0:T(8,128)} %get-tuple-element.11), channel_id=1, source_target_pairs={{0,1},{1,0},{2,3},{3,2},{4,5},{5,4},{6,7},{7,6},{8,9},{9,8},{10,11... | collective-permute-start | bytes 393224 | tf_op jit(solution)/shard_map/ppermute | solution.py:540
  24.0 1.2 collective-permute-done
  25.2 0.9 add.3
  26.2 42.4 %all_to_all.20 = f32[32,8,128]{2,1,0:T(8,128)S(1)} all-to-all(f32[32,8,128]{2,1,0:T(8,128)S(1)} %add.3), channel_id=1, replica_groups=mesh['groups'=4,'gx'=32,'gy'=2] {'gx'}, dimensions={0} | all-to-all | bytes 262144 | tf_op jit(solution)/shard_map/all_to_all | solution.py:503
  68.6 0.9 copy-done.4
  69.5 0.8 shard_map.110
  70.3 4.8 %all-to-all-start.1 = ((f32[32,4,128]{2,1,0:T(4,128)}), f32[32,4,128]{2,1,0:T(4,128)S(1)}, u32[]{:S(2)}, u32[]{:S(2)}) async-start(f32[32,4,128]{2,1,0:T(4,128)} %bitcast.2), calls=%async_computation.1 | async-start | bytes 131072 | tf_op jit(solution)/shard_map/all_to_all | solution.py:503
  75.1 0.0 copy-start
  75.1 3.4 %copy-done = f32[16,1,16,2,32,32]{5,4,3,2,1,0:T(8,128)S(1)} copy-done((f32[16,1,16,2,32,32]{5,4,3,2,1,0:T(8,128)S(1)}, f32[16,1,16,2,32,32]{5,4,3,2,1,0:T(8,128)}, u32[]{:S(2)}) %copy-start) | copy-done | bytes 2097176
  78.5 10.1 %shard_map.111.weight_ref = f32[2,2,32,32,128]{4,3,2,1,0:T(8,128)S(1)} custom-call(f32[16384,32]{1,0:T(8,128)S(1)} %bitcast.12), custom_call_target="tpu_custom_call" | custom-call | flops 1073741824 | bytes 10485760 | tf_op jit(solution)/shard_map/pallas_call | solution.py:553
  88.5 9.1 %all-to-all-done.1 = f32[32,4,128]{2,1,0:T(4,128)S(1)} async-done(((f32[32,4,128]{2,1,0:T(4,128)}), f32[32,4,128]{2,1,0:T(4,128)S(1)}, u32[]{:S(2)}, u32[]{:S(2)}) %all-to-all-start.1) | async-done | bytes 65568 | tf_op jit(solution)/shard_map/all_to_all | solution.py:503
  97.7 1.3 shard_map.112
  98.9 12.3 %all-to-all-start.2 = ((f32[32,4,128]{2,1,0:T(4,128)}), f32[32,4,128]{2,1,0:T(4,128)S(1)}, u32[]{:S(2)}, u32[]{:S(2)}) async-start(f32[32,4,128]{2,1,0:T(4,128)} %bitcast.5), calls=%async_computation.2 | async-start | bytes 131072 | tf_op jit(solution)/shard_map/all_to_all | solution.py:503
  111.2 2.3 %collective-permute-start.2 = (f32[2,32,2048]{2,1,0:T(8,128)S(1)}, f32[2,32,2048]{2,1,0:T(8,128)S(1)}, u32[]{:S(2)}, u32[]{:S(2)}) collective-permute-start(f32[2,32,2048]{2,1,0:T(8,128)S(1)} %copy-done.1), channel_id=1, source_target_pairs={{2,0},{4,2},{6,4},{8,6},{10,8},{12,10},{14,12},{16,14},{18,16},{20... | collective-permute-start | bytes 1572872 | tf_op jit(solution)/shard_map/ppermute | solution.py:544
  113.6 20.4 %all-to-all-done.2 = f32[32,4,128]{2,1,0:T(4,128)S(1)} async-done(((f32[32,4,128]{2,1,0:T(4,128)}), f32[32,4,128]{2,1,0:T(4,128)S(1)}, u32[]{:S(2)}, u32[]{:S(2)}) %all-to-all-start.2) | async-done | bytes 65568 | tf_op jit(solution)/shard_map/all_to_all | solution.py:503
  133.9 0.9 shard_map.113
  134.8 4.8 %all-to-all-start.3 = ((f32[32,8,128]{2,1,0:T(8,128)}), f32[32,8,128]{2,1,0:T(8,128)S(1)}, u32[]{:S(2)}, u32[]{:S(2)}) async-start(f32[32,8,128]{2,1,0:T(8,128)} %bitcast.7), calls=%async_computation.3 | async-start | bytes 262144 | tf_op jit(solution)/shard_map/all_to_all | solution.py:503
  139.7 4.4 %collective-permute-start.3 = (f32[4,2048]{1,0:T(4,128)S(1)}, f32[4,2048]{1,0:T(4,128)S(1)}, u32[]{:S(2)}, u32[]{:S(2)}) collective-permute-start(f32[4,2048]{1,0:T(4,128)S(1)} %shard_map.114), channel_id=1, source_target_pairs={{0,1},{1,0},{2,3},{3,2},{4,5},{5,4},{6,7},{7,6},{8,9},{9,8},{10,11... | collective-permute-start | bytes 98312 | tf_op jit(solution)/shard_map/ppermute | solution.py:474
  144.1 0.9 collective-permute-done.3.rim_ref
  145.0 9.0 %shard_map.115.second_top.second_end.second_ref = f32[2,32,2048]{2,1,0:T(8,128)S(1)} custom-call(f32[2,32,2048]{2,1,0:T(8,128)S(1)} %copy-done.1, f32[2,32,2048]{2,1,0:T(8,128)S(1)} %collective-permute-done.2.second_top.second_end.second_ref, f32[4,2048]{1,0:T(4,128)S(1)} %collective-permute-done.3.rim_ref, f32[9,96,32]{2,1,0:T(8,128)S(1)} %bitcast.18), custom_call_target="tpu_custom_call" | custom-call | flops 3623878656 | bytes 2097152 | tf_op jit(solution)/shard_map/pallas_call | solution.py:482
  153.9 0.0 copy-start.2
  153.9 0.0 copy-start.5
  154.0 0.8 collective-permute-start.4
  154.8 15.3 %collective-permute-done.4.first_top.first_end.first_ref = f32[2,32,2048]{2,1,0:T(8,128)S(1)} collective-permute-done((f32[2,32,2048]{2,1,0:T(8,128)S(1)}, f32[2,32,2048]{2,1,0:T(8,128)S(1)}, u32[]{:S(2)}, u32[]{:S(2)}) %collective-permute-start.4) | collective-permute-done | bytes 524320 | tf_op jit(solution)/shard_map/ppermute | solution.py:569
  170.2 1.0 collective-permute-start.5
  171.2 0.1 reshape_tile.3.bias_ref
  171.3 0.2 collective-permute-start.1
  171.5 0.6 collective-permute-done.5.rim_ref
  172.1 8.9 %shard_map.117 = f32[2,32,2048]{2,1,0:T(8,128)S(1)} custom-call(f32[2,32,2048]{2,1,0:T(8,128)S(1)} %collective-permute-done.4.first_top.first_end.first_ref, f32[2,32,2048]{2,1,0:T(8,128)S(1)} %shard_map.115.second_top.second_end.second_ref, f32[4,2048]{1,0:T(4,128)S(1)} %collective-permute-done.5.rim_ref, f32[9,96,32]{2,1,0:T(8,128)S(1)} %bitcast.19), custom_call_target="tpu_custom_call" | custom-call | flops 3623878656 | bytes 2097152 | tf_op jit(solution)/shard_map/pallas_call | solution.py:482
  181.0 2.8 %shard_map.118 = f32[64,2048]{1,0:T(8,128)} custom-call(f32[32,8,128]{2,1,0:T(8,128)S(1)} %all-to-all-done.3.own_ref, f32[32,8,128]{2,1,0:T(8,128)S(1)} %collective-permute-done.1.other_ref, bf16[2,2,2,128,64]{4,3,2,1,0:T(8,128)(2,1)S(1)} %copy-done.2, f32[2,16,128]{2,1,0:T(8,128)S(1)} %copy-done.5, f32[64,2048]{1,0:T(8,128)S(1)} %bitcast.14, ...), custom_call_target="tpu_custom_call" | custom-call | tf_op jit(solution)/shard_map/pallas_call | solution.py:576
  (18 shorter events, 0.1 us)
Async XLA Ops:
  0.0 133.9 %copy-start.3 = (bf16[2,256,128]{2,1,0:T(8,128)(2,1)S(1)}, bf16[2,256,128]{2,1,0:T(8,128)(2,1)}, u32[]{:S(2)}) copy-start(bf16[2,256,128]{2,1,0:T(8,128)(2,1)} %constant.15.clone.table_ref) | copy-start | bytes 393220
  0.0 111.2 %copy-start.1 = (f32[2,32,2048]{2,1,0:T(8,128)S(1)}, f32[2,32,2048]{2,1,0:T(8,128)}, u32[]{:S(2)}) copy-start(f32[2,32,2048]{2,1,0:T(8,128)} %first_ref) | copy-start | bytes 1572868
  3.5 141.5 %copy-start.6 = (f32[3,3,3,32,32]{4,3,2,1,0:T(8,128)S(1)}, f32[3,3,3,32,32]{4,3,2,1,0:T(8,128)}, u32[]{:S(2)}) copy-start(f32[3,3,3,32,32]{4,3,2,1,0:T(8,128)} %param.13) | copy-start | bytes 331780
  3.5 21.7 %collective-permute-start = (f32[32,8,128]{2,1,0:T(8,128)}, f32[32,8,128]{2,1,0:T(8,128)S(1)}, u32[]{:S(2)}, u32[]{:S(2)}) collective-permute-start(f32[32,8,128]{2,1,0:T(8,128)} %get-tuple-element.11), channel_id=1, source_target_pairs={{0,1},{1,0},{2,3},{3,2},{4,5},{5,4},{6,7},{7,6},{8,9},{9,8},{10,11... | collective-permute-start | bytes 393224 | tf_op jit(solution)/shard_map/ppermute | solution.py:540
  68.6 0.9 copy-start.4
  70.3 27.4 %all-to-all-start.1 = ((f32[32,4,128]{2,1,0:T(4,128)}), f32[32,4,128]{2,1,0:T(4,128)S(1)}, u32[]{:S(2)}, u32[]{:S(2)}) async-start(f32[32,4,128]{2,1,0:T(4,128)} %bitcast.2), calls=%async_computation.1 | async-start | bytes 131072 | tf_op jit(solution)/shard_map/all_to_all | solution.py:503
  75.1 3.4 %copy-start = (f32[16,1,16,2,32,32]{5,4,3,2,1,0:T(8,128)S(1)}, f32[16,1,16,2,32,32]{5,4,3,2,1,0:T(8,128)}, u32[]{:S(2)}) copy-start(f32[16,1,16,2,32,32]{5,4,3,2,1,0:T(8,128)} %param.12) | copy-start | bytes 6291460
  98.9 35.0 %all-to-all-start.2 = ((f32[32,4,128]{2,1,0:T(4,128)}), f32[32,4,128]{2,1,0:T(4,128)S(1)}, u32[]{:S(2)}, u32[]{:S(2)}) async-start(f32[32,4,128]{2,1,0:T(4,128)} %bitcast.5), calls=%async_computation.2 | async-start | bytes 131072 | tf_op jit(solution)/shard_map/all_to_all | solution.py:503
  111.2 28.4 %collective-permute-start.2 = (f32[2,32,2048]{2,1,0:T(8,128)S(1)}, f32[2,32,2048]{2,1,0:T(8,128)S(1)}, u32[]{:S(2)}, u32[]{:S(2)}) collective-permute-start(f32[2,32,2048]{2,1,0:T(8,128)S(1)} %copy-done.1), channel_id=1, source_target_pairs={{2,0},{4,2},{6,4},{8,6},{10,8},{12,10},{14,12},{16,14},{18,16},{20... | collective-permute-start | bytes 1572872 | tf_op jit(solution)/shard_map/ppermute | solution.py:544
  134.8 36.5 %all-to-all-start.3 = ((f32[32,8,128]{2,1,0:T(8,128)}), f32[32,8,128]{2,1,0:T(8,128)S(1)}, u32[]{:S(2)}, u32[]{:S(2)}) async-start(f32[32,8,128]{2,1,0:T(8,128)} %bitcast.7), calls=%async_computation.3 | async-start | bytes 262144 | tf_op jit(solution)/shard_map/all_to_all | solution.py:503
  139.6 31.6 %copy-start.8 = (f32[32]{0:T(128)S(1)}, f32[32]{0:T(128)}, u32[]{:S(2)}) copy-start(f32[32]{0:T(128)} %param.15) | copy-start | bytes 388
  139.6 32.5 %copy-start.7 = (f32[3,3,3,32,32]{4,3,2,1,0:T(8,128)S(1)}, f32[3,3,3,32,32]{4,3,2,1,0:T(8,128)}, u32[]{:S(2)}) copy-start(f32[3,3,3,32,32]{4,3,2,1,0:T(8,128)} %param.14) | copy-start | bytes 331780
  139.7 5.3 %collective-permute-start.3 = (f32[4,2048]{1,0:T(4,128)S(1)}, f32[4,2048]{1,0:T(4,128)S(1)}, u32[]{:S(2)}, u32[]{:S(2)}) collective-permute-start(f32[4,2048]{1,0:T(4,128)S(1)} %shard_map.114), channel_id=1, source_target_pairs={{0,1},{1,0},{2,3},{3,2},{4,5},{5,4},{6,7},{7,6},{8,9},{9,8},{10,11... | collective-permute-start | bytes 98312 | tf_op jit(solution)/shard_map/ppermute | solution.py:474
  153.9 27.0 %copy-start.2 = (bf16[2,2,2,128,64]{4,3,2,1,0:T(8,128)(2,1)S(1)}, bf16[2,2,2,128,64]{4,3,2,1,0:T(8,128)(2,1)}, u32[]{:S(2)}) copy-start(bf16[2,2,2,128,64]{4,3,2,1,0:T(8,128)(2,1)} %constant.16.clone.table_ref) | copy-start | bytes 393220
  153.9 27.0 %copy-start.5 = (f32[2,16,128]{2,1,0:T(8,128)S(1)}, f32[2,16,128]{2,1,0:T(8,128)}, u32[]{:S(2)}) copy-start(f32[2,16,128]{2,1,0:T(8,128)} %constant.17.clone.twiddle_ref) | copy-start | bytes 49156
  154.0 16.2 %collective-permute-start.4 = (f32[2,32,2048]{2,1,0:T(8,128)S(1)}, f32[2,32,2048]{2,1,0:T(8,128)S(1)}, u32[]{:S(2)}, u32[]{:S(2)}) collective-permute-start(f32[2,32,2048]{2,1,0:T(8,128)S(1)} %shard_map.115.second_top.second_end.second_ref), channel_id=1, source_target_pairs={{0,2},{2,4},{4,6},{6,8},{8,10},{10,12},{12,14},{14,16},{16,18},{18... | collective-permute-start | bytes 1572872 | tf_op jit(solution)/shard_map/ppermute | solution.py:569
  170.2 1.9 %collective-permute-start.5 = (f32[4,2048]{1,0:T(4,128)S(1)}, f32[4,2048]{1,0:T(4,128)S(1)}, u32[]{:S(2)}, u32[]{:S(2)}) collective-permute-start(f32[4,2048]{1,0:T(4,128)S(1)} %shard_map.116), channel_id=1, source_target_pairs={{0,1},{1,0},{2,3},{3,2},{4,5},{5,4},{6,7},{7,6},{8,9},{9,8},{10,11... | collective-permute-start | bytes 98312 | tf_op jit(solution)/shard_map/ppermute | solution.py:474
  171.3 9.7 %collective-permute-start.1 = (f32[32,8,128]{2,1,0:T(8,128)S(1)}, f32[32,8,128]{2,1,0:T(8,128)S(1)}, u32[]{:S(2)}, u32[]{:S(2)}) collective-permute-start(f32[32,8,128]{2,1,0:T(8,128)S(1)} %all-to-all-done.3.own_ref), channel_id=1, source_target_pairs={{0,1},{1,0},{2,3},{3,2},{4,5},{5,4},{6,7},{7,6},{8,9},{9,8},{10,11... | collective-permute-start | bytes 393224 | tf_op jit(solution)/shard_map/ppermute | solution.py:575

commit v3 on v2

--- a/solution.py
+++ b/solution.py
@@ -126,39 +126,22 @@
     return out
 
 
-def forward_kernel(
-    cells_hbm, table_hbm, twiddle_hbm, keep_ref, send_ref, z_ref, cells_ref, table_ref,
-    twiddle_ref, sems, *, devices_y,
-):
+def forward_kernel(cells_ref, table_ref, keep_ref, send_ref, z_ref, *, devices_y):
     rows = cells_ref.shape[0]
     here = lax.axis_index("gy")
     there = devices_y - 1 - here
+    size = keep_ref.shape[0] * ROWS // (MZ // GROUP)
+    twiddles = devices_y * devices_y * size
     lane = lax.broadcasted_iota(jnp.int32, (ROWS, LANES), 1)
-    half_rows = rows // 2
-    twiddle_copy = pltpu.make_async_copy(twiddle_hbm, twiddle_ref, sems.at[0])
-    table_copy = pltpu.make_async_copy(table_hbm.at[here], table_ref, sems.at[1])
-    cell_copies = [
-        pltpu.make_async_copy(
-            cells_hbm.at[pl.ds(part * half_rows, half_rows)],
-            cells_ref.at[pl.ds(part * half_rows, half_rows)],
-            sems.at[2 + part],
-        )
-        for part in range(2)
-    ]
-    twiddle_copy.start()
-    cell_copies[0].start()
-    cell_copies[1].start()
-    table_copy.start()
-    twiddle_copy.wait()
 
     def step(i, carry):
         start = pl.multiple_of(i * ROWS, ROWS)
         blocks = [cells_ref[pl.ds(start, ROWS), q * LANES : (q + 1) * LANES] for q in range(ZQ)]
 
         def twiddle(k):
-            return (
-                jnp.broadcast_to(twiddle_ref[0, k : k + 1, :], (ROWS, LANES)),
-                jnp.broadcast_to(twiddle_ref[1, k : k + 1, :], (ROWS, LANES)),
+            return tuple(
+                jnp.broadcast_to(table_ref[row : row + 1, :], (ROWS, LANES))
+                for row in (twiddles + k, twiddles + MZ + k)
             )
 
         real, imag = z_forward(blocks, twiddle, lane)
@@ -167,15 +150,12 @@
             z_ref[pl.ds(start + rows, ROWS), h * LANES : (h + 1) * LANES] = imag[h]
         return carry
 
-    steps = half_rows // ROWS
-    for part in range(2):
-        cell_copies[part].wait()
-        lax.fori_loop(part * steps, (part + 1) * steps, step, 0)
-    table_copy.wait()
+    lax.fori_loop(0, rows // ROWS, step, 0)
     high, low = split(z_ref[...])
     for target, out_ref in ((there, send_ref), (here, keep_ref)):
-        table = table_ref[target, 0]
-        modes = dot(table, high) + (dot(table_ref[target, 1], high) + dot(table, low))
+        first = pl.multiple_of((here * devices_y + target) * size, size)
+        table, table_low = split(table_ref[pl.ds(first, size), :])
+        modes = dot(table, high) + (dot(table_low, high) + dot(table, low))
         for h in range(MZ // GROUP):
             for kp in range(modes.shape[0] // ROWS):
                 out_ref[h * (modes.shape[0] // ROWS) + kp] = modes[
@@ -215,60 +195,65 @@
     )(table, value)
 
 
-def arrange_kernel(weight_ref, out_ref, *, owned_y):
-    halves, channels = out_ref.shape[1:3]
-    wide = MZ // GROUP
-    per = GROUP // halves
-    stride = MZ * 2 * channels
-
-    def step(c, carry):
-        for part in range(2):
-            for h in range(halves):
-                pieces = []
-                for g in range(per):
-                    for block in range(wide):
-                        kz = block * GROUP + h * per + g
-                        first = (kz * 2 + part) * channels + c
-                        pieces.append(weight_ref[pl.ds(first, owned_y, stride=stride), :])
-                out_ref[part, h, c] = jnp.concatenate(pieces, axis=0).T
+def prepare_kernel(weight_ref, high_ref, low_ref):
+    depth = high_ref.shape[2]
+
+    def step(i, carry):
+        for block in range(MZ // GROUP):
+            first = block * GROUP * depth
+            value = jnp.concatenate(
+                [
+                    weight_ref[i, first + g * depth : first + (g + 1) * depth, :]
+                    for g in range(GROUP)
+                ],
+                axis=1,
+            )
+            high_ref[block, i], low_ref[block, i] = split(value)
         return carry
 
-    lax.fori_loop(0, channels, step, 0)
-
-
-def mix_kernel(modes_ref, weight_ref, out_ref):
-    count = modes_ref.shape[0] // 2
-    halves = GROUP * count // LANES
-    per = GROUP // halves
-    parts = []
-    for part in range(2):
-        turned = modes_ref[pl.ds(part, count, stride=2), :].T
-        parts.append(
-            [
-                jnp.concatenate(
-                    [turned[(h * per + g) * CH : (h * per + g + 1) * CH] for g in range(per)],
-                    axis=1,
-                )
-                for h in range(halves)
-            ]
-        )
-    outs = ([], [])
-    for h in range(halves):
-        re, im = parts[0][h], parts[1][h]
-        acc_re = jnp.zeros((CH, LANES), F32)
-        acc_im = jnp.zeros((CH, LANES), F32)
-        for c in range(CH):
-            wr = weight_ref[0, h, c]
-            wi = weight_ref[1, h, c]
-            a = re[c : c + 1, :]
-            b = im[c : c + 1, :]
-            acc_re = acc_re + (a * wr - b * wi)
-            acc_im = acc_im + (a * wi + b * wr)
-        for g in range(per):
-            outs[0].append(acc_re[:, g * count : (g + 1) * count])
-            outs[1].append(acc_im[:, g * count : (g + 1) * count])
-    for part in range(2):
-        out_ref[pl.ds(part, count, stride=2), :] = jnp.concatenate(outs[part], axis=0).T
+    lax.fori_loop(0, weight_ref.shape[0], step, 0)
+
+
+def mix_kernel(modes_ref, weight_high_ref, weight_low_ref, out_ref):
+    owned_y, depth = weight_high_ref.shape[1:3]
+    channels = depth // 2
+    span = owned_y * depth
+    repeats = span // LANES
+    lane = lax.broadcasted_iota(jnp.int32, (owned_y, LANES), 1)
+    group = lane // channels
+    second = group % 2 == 1
+    both_group = lax.broadcasted_iota(jnp.int32, (2 * owned_y, LANES), 1) // channels
+    wide_lane = lax.broadcasted_iota(jnp.int32, (2 * owned_y, span), 1)
+    wide_row = lax.broadcasted_iota(jnp.int32, (2 * owned_y, span), 0)
+    own = wide_lane // depth == wide_row % owned_y
+
+    def spread(value, g):
+        value = jnp.where(group == g, value, 0.0)
+        value = value + pltpu.roll(value, LANES // 2, 1)
+        return value + pltpu.roll(value, channels, 1)
+
+    for block in range(MZ // GROUP):
+        first = block * 2 * owned_y
+        real = modes_ref[pl.ds(first, owned_y, stride=2), :]
+        imag = modes_ref[pl.ds(first + 1, owned_y, stride=2), :]
+        left = ([], [])
+        for g in range(GROUP):
+            re, im = spread(real, g), spread(imag, g)
+            pair = jnp.concatenate([jnp.where(second, -im, re), jnp.where(second, re, im)], axis=0)
+            for part, value in zip(left, split(pair), strict=True):
+                wide = jnp.concatenate([value.astype(F32)] * repeats, axis=1)
+                part.append(jnp.where(own, wide, 0.0).astype(BF16))
+        high, low = (jnp.concatenate(part, axis=0) for part in left)
+        weight_high = weight_high_ref[block].reshape(span, LANES)
+        weight_low = weight_low_ref[block].reshape(span, LANES)
+        total = dot(high, weight_high) + (dot(low, weight_high) + dot(high, weight_low))
+        mixed = total[: 2 * owned_y]
+        for g in range(1, GROUP):
+            mixed = jnp.where(
+                both_group == g, total[g * 2 * owned_y : (g + 1) * 2 * owned_y], mixed
+            )
+        out_ref[pl.ds(first, owned_y, stride=2), :] = mixed[:owned_y]
+        out_ref[pl.ds(first + 1, owned_y, stride=2), :] = mixed[owned_y:]
 
 
 def inverse_tables(cells_x, cells_y, devices_y):
@@ -515,7 +500,12 @@
     tiles = owned_y // pair * wide
     assert devices_y == 2 and cells_x == 2 and tiles == devices_x and MX == devices_x
 
-    forward_y = np.moveaxis(host_split(forward_tables(cells_x, cells_y, devices_y)), 0, 2)
+    forward_y = np.concatenate(
+        [
+            forward_tables(cells_x, cells_y, devices_y).reshape(-1, 2 * cells_x * cells_y),
+            z_twiddle(-1).reshape(-1, LANES),
+        ]
+    ).astype(np.float32)
     inverse_y = np.moveaxis(host_split(inverse_tables(cells_x, cells_y, devices_y)), 0, 2)
     forward_x, inverse_x = (host_split(t) for t in x_tables(cells_x, devices_x, pair))
     twiddle_out = z_twiddle(1)
@@ -526,19 +516,13 @@
     keep, send = pl.pallas_call(
         functools.partial(forward_kernel, devices_y=devices_y),
         out_shape=(tile_shape, tile_shape),
-        in_specs=[pl.BlockSpec(memory_space=pltpu.HBM)] * 3,
+        in_specs=[VMEM] * 2,
         out_specs=(VMEM, VMEM),
-        scratch_shapes=[
-            pltpu.VMEM((2 * cells_x * cells_y, MZ * CH), F32),
-            pltpu.VMEM((cells_x * cells_y, width), F32),
-            pltpu.VMEM(forward_y.shape[1:], BF16),
-            pltpu.VMEM((2, MZ, LANES), F32),
-            pltpu.SemaphoreType.DMA((4,)),
-        ],
-        compiler_params=pltpu.CompilerParams(vmem_limit_bytes=58 << 20),
-    )(field.reshape(cells_x * cells_y, width), forward_y, z_twiddle(-1))
+        scratch_shapes=[pltpu.VMEM((2 * cells_x * cells_y, MZ * CH), F32)],
+        compiler_params=small_grant(),
+    )(field.reshape(cells_x * cells_y, width), forward_y)
     lines = keep + lax.ppermute(send, "gy", [(0, 1), (1, 0)])
-    lines, cells, spectral = lax.optimization_barrier((lines, field, spectral))
+    lines, cells = lax.optimization_barrier((lines, field))
 
     columns = all_to_all(lines)
     following = lax.ppermute(
@@ -549,22 +533,22 @@
     modes = all_to_all(modes.reshape(MX, 2 * pair, LANES))
 
     count = tiles * pair
-    halves = GROUP * count // LANES
+    matrix_shape = (wide, owned_y, 2 * CH, LANES)
     matrix = pl.pallas_call(
-        functools.partial(arrange_kernel, owned_y=owned_y),
-        out_shape=jax.ShapeDtypeStruct((2, halves, CH, CH, LANES), F32),
+        prepare_kernel,
+        out_shape=(jax.ShapeDtypeStruct(matrix_shape, BF16),) * 2,
         in_specs=[VMEM],
-        out_specs=VMEM,
-        compiler_params=pltpu.CompilerParams(vmem_limit_bytes=24 << 20),
-        cost_estimate=pl.CostEstimate(flops=1 << 30, transcendentals=0, bytes_accessed=10 << 20),
-    )(spectral.reshape(-1, CH))
+        out_specs=(VMEM, VMEM),
+        compiler_params=pltpu.CompilerParams(vmem_limit_bytes=20 << 20),
+        cost_estimate=pl.CostEstimate(flops=1 << 28, transcendentals=0, bytes_accessed=16 << 20),
+    )(spectral.reshape(owned_y, MZ * 2 * CH, CH))
     mixed = pl.pallas_call(
         mix_kernel,
         out_shape=jax.ShapeDtypeStruct((2 * count, LANES), F32),
-        in_specs=[VMEM, VMEM],
+        in_specs=[VMEM] * 3,
         out_specs=VMEM,
-        compiler_params=small_grant(),
-    )(modes.reshape(2 * count, LANES), matrix)
+        compiler_params=pltpu.CompilerParams(vmem_limit_bytes=20 << 20),
+    )(modes.reshape(2 * count, LANES), *matrix)
     columns = all_to_all(mixed.reshape(tiles, 2 * pair, LANES))
     previous = lax.ppermute(
         hidden, "gx", [(i, (i + 1) % devices_x) for i in range(devices_x)]

time: 184 us -> 177 us (0.962)
  Pallas kernels: 37.2 us -> 28.7 us
  waiting for transfers between devices: 47.5 us -> 54.6 us
  starting transfers between devices: 51.1 us -> 44.1 us
  local copies, waits for them, and re-layouts: 4.41 us -> 6.36 us
    pallas_call x1, Pallas kernels: 10.1 us -> 2.76 us  [block(): pl.pallas_call(prepare_kernel, out_shape=(jax.ShapeDtypeStruct(matrix_sha...]
    all_to_all x3, starting transfers between devices: 21.8 us -> 14.5 us  [all_to_all(): return lax.all_to_all(value, 'gx', split_axis=0, concat_axis=0, tiled=True)]
    all_to_all x3, waiting for transfers between devices: 29.5 us -> 36.8 us  [all_to_all(): return lax.all_to_all(value, 'gx', split_axis=0, concat_axis=0, tiled=True)]
    unnamed x18 -> x22, local copies, waits for them, and re-layouts: 4.32 us -> 6.27 us
  transfers between devices with their start and end apart: 9 -> 9, of which waited for: 6 -> 6; matrix products, arithmetic and copies ran while one was open for 0% -> 0% of each run, Pallas kernels for 16% -> 12%
where the time goes in v3:
time: 177 us; the launch traced here: 176 us
  waiting for transfers between devices  54.6 us (31%)
  starting transfers between devices  44.1 us (25%)
  blocking collectives  42.4 us (24%)
  Pallas kernels  28.7 us (16%)
  local copies, waits for them, and re-layouts  6.36 us (4%)
    all_to_all x1, blocking collectives, all_to_all(): return lax.all_to_all(value, 'gx', split_axis=0, concat_axis=0, tiled=True)  42.4 us
    all_to_all x3, waiting for transfers between devices, all_to_all(): return lax.all_to_all(value, 'gx', split_axis=0, concat_axis=0, tiled=True)  36.8 us
    ppermute x1, starting transfers between devices, block(): lines = keep + lax.ppermute(send, 'gy', [(0, 1), (1, 0)])  20.5 us
    pallas_call x2, Pallas kernels, band_product(): pl.pallas_call(functools.partial(conv_kernel, shifted=shifted, activate=a...  17.9 us
    ppermute x1, waiting for transfers between devices, block(): lax.ppermute(hidden, 'gx', [(i, (i + 1) % devices_x) for i in range(devic...  15.3 us
    all_to_all x3, starting transfers between devices, all_to_all(): return lax.all_to_all(value, 'gx', split_axis=0, concat_axis=0, tiled=True)  14.5 us
    unnamed x22, local copies, waits for them, and re-layouts  6.27 us
    ppermute x2, starting transfers between devices, convolve(): rim = lax.ppermute(rim, 'gy', [(0, 1), (1, 0)])  5.76 us
  transfers between devices with their start and end apart: 9, of which 6 were waited for; matrix products, arithmetic and copies ran while one was open for 0% of the time, Pallas kernels for 12%

profile of v3, /device:TPU:37, one launch (start us, length us, event | category | flops | bytes accessed | tf_op | source)
XLA Modules:
  0.0 176.3 jit_solution(6754211954936114682)
XLA Ops:
  0.0 1.0 copy-done.1
  1.0 0.9 copy-done.4
  2.0 1.7 shard_map.100
  3.7 20.5 %collective-permute-start = (f32[32,8,128]{2,1,0:T(8,128)S(1)}, f32[32,8,128]{2,1,0:T(8,128)S(1)}, u32[]{:S(2)}, u32[]{:S(2)}) collective-permute-start(f32[32,8,128]{2,1,0:T(8,128)S(1)} %get-tuple-element.12), channel_id=1, source_target_pairs={{0,1},{1,0},{2,3},{3,2},{4,5},{5,4},{6,7},{7,6},{8,9},{9,8},{10,11... | collective-permute-start | bytes 393224 | tf_op jit(solution)/shard_map/ppermute | solution.py:524
  24.3 1.0 collective-permute-done
  25.3 42.4 %all_to_all.20 = f32[32,8,128]{2,1,0:T(8,128)S(1)} all-to-all(f32[32,8,128]{2,1,0:T(8,128)S(1)} %add.3), channel_id=1, replica_groups=mesh['groups'=4,'gx'=32,'gy'=2] {'gx'}, dimensions={0} | all-to-all | bytes 262144 | tf_op jit(solution)/shard_map/all_to_all | solution.py:488
  67.7 0.9 copy-done.6
  68.6 0.8 shard_map.101
  69.4 4.8 %all-to-all-start.1 = ((f32[32,4,128]{2,1,0:T(4,128)}), f32[32,4,128]{2,1,0:T(4,128)S(1)}, u32[]{:S(2)}, u32[]{:S(2)}) async-start(f32[32,4,128]{2,1,0:T(4,128)} %bitcast.2), calls=%async_computation.1 | async-start | bytes 131072 | tf_op jit(solution)/shard_map/all_to_all | solution.py:488
  74.2 3.4 %copy-done = f32[16,1,16,2,32,32]{5,4,3,2,1,0:T(8,128)S(1)} copy-done((f32[16,1,16,2,32,32]{5,4,3,2,1,0:T(8,128)S(1)}, f32[16,1,16,2,32,32]{5,4,3,2,1,0:T(8,128)}, u32[]{:S(2)}) %copy-start) | copy-done | bytes 2097176
  77.5 2.8 %shard_map.102 = (bf16[4,16,64,128]{3,2,1,0:T(8,128)(2,1)S(1)}, bf16[4,16,64,128]{3,2,1,0:T(8,128)(2,1)S(1)}) custom-call(f32[16,1024,32]{2,1,0:T(8,128)S(1)} %bitcast.12), custom_call_target="tpu_custom_call" | custom-call | flops 268435456 | bytes 16777216 | tf_op jit(solution)/shard_map/pallas_call | solution.py:537
  80.3 16.5 %all-to-all-done.1 = f32[32,4,128]{2,1,0:T(4,128)S(1)} async-done(((f32[32,4,128]{2,1,0:T(4,128)}), f32[32,4,128]{2,1,0:T(4,128)S(1)}, u32[]{:S(2)}, u32[]{:S(2)}) %all-to-all-start.1) | async-done | bytes 65568 | tf_op jit(solution)/shard_map/all_to_all | solution.py:488
  96.8 1.8 shard_map.103
  98.5 5.0 %all-to-all-start.2 = ((f32[32,4,128]{2,1,0:T(4,128)}), f32[32,4,128]{2,1,0:T(4,128)S(1)}, u32[]{:S(2)}, u32[]{:S(2)}) async-start(f32[32,4,128]{2,1,0:T(4,128)} %bitcast.5), calls=%async_computation.2 | async-start | bytes 131072 | tf_op jit(solution)/shard_map/all_to_all | solution.py:488
  103.5 2.3 %collective-permute-start.2 = (f32[2,32,2048]{2,1,0:T(8,128)S(1)}, f32[2,32,2048]{2,1,0:T(8,128)S(1)}, u32[]{:S(2)}, u32[]{:S(2)}) collective-permute-start(f32[2,32,2048]{2,1,0:T(8,128)S(1)} %copy-done.2), channel_id=1, source_target_pairs={{2,0},{4,2},{6,4},{8,6},{10,8},{12,10},{14,12},{16,14},{18,16},{20... | collective-permute-start | bytes 1572872 | tf_op jit(solution)/shard_map/ppermute | solution.py:528
  105.9 20.4 %all-to-all-done.2 = f32[32,4,128]{2,1,0:T(4,128)S(1)} async-done(((f32[32,4,128]{2,1,0:T(4,128)}), f32[32,4,128]{2,1,0:T(4,128)S(1)}, u32[]{:S(2)}, u32[]{:S(2)}) %all-to-all-start.2) | async-done | bytes 65568 | tf_op jit(solution)/shard_map/all_to_all | solution.py:488
  126.2 0.9 shard_map.104
  127.1 4.8 %all-to-all-start.3 = ((f32[32,8,128]{2,1,0:T(8,128)}), f32[32,8,128]{2,1,0:T(8,128)S(1)}, u32[]{:S(2)}, u32[]{:S(2)}) async-start(f32[32,8,128]{2,1,0:T(8,128)} %bitcast.7), calls=%async_computation.3 | async-start | bytes 262144 | tf_op jit(solution)/shard_map/all_to_all | solution.py:488
  131.8 0.0 copy-start.10
  131.9 4.7 %collective-permute-start.3 = (f32[4,2048]{1,0:T(4,128)S(1)}, f32[4,2048]{1,0:T(4,128)S(1)}, u32[]{:S(2)}, u32[]{:S(2)}) collective-permute-start(f32[4,2048]{1,0:T(4,128)S(1)} %shard_map.105), channel_id=1, source_target_pairs={{0,1},{1,0},{2,3},{3,2},{4,5},{5,4},{6,7},{7,6},{8,9},{9,8},{10,11... | collective-permute-start | bytes 98312 | tf_op jit(solution)/shard_map/ppermute | solution.py:459
  136.7 0.9 collective-permute-done.3.rim_ref
  137.5 9.0 %shard_map.106.second_top.second_end.second_ref = f32[2,32,2048]{2,1,0:T(8,128)S(1)} custom-call(f32[2,32,2048]{2,1,0:T(8,128)S(1)} %copy-done.2, f32[2,32,2048]{2,1,0:T(8,128)S(1)} %collective-permute-done.2.second_top.second_end.second_ref, f32[4,2048]{1,0:T(4,128)S(1)} %collective-permute-done.3.rim_ref, f32[9,96,32]{2,1,0:T(8,128)S(1)} %bitcast.18), custom_call_target="tpu_custom_call" | custom-call | flops 3623878656 | bytes 2097152 | tf_op jit(solution)/shard_map/pallas_call | solution.py:467
  146.5 0.0 copy-start.3
  146.5 0.0 copy-start.7
  146.5 0.8 collective-permute-start.4
  147.4 15.3 %collective-permute-done.4.first_top.first_end.first_ref = f32[2,32,2048]{2,1,0:T(8,128)S(1)} collective-permute-done((f32[2,32,2048]{2,1,0:T(8,128)S(1)}, f32[2,32,2048]{2,1,0:T(8,128)S(1)}, u32[]{:S(2)}, u32[]{:S(2)}) %collective-permute-start.4) | collective-permute-done | bytes 524320 | tf_op jit(solution)/shard_map/ppermute | solution.py:553
  162.7 1.0 collective-permute-start.5
  163.7 0.1 reshape_tile.3.bias_ref
  163.8 0.1 collective-permute-start.1
  163.9 0.7 collective-permute-done.5.rim_ref
  164.6 8.9 %shard_map.108 = f32[2,32,2048]{2,1,0:T(8,128)S(1)} custom-call(f32[2,32,2048]{2,1,0:T(8,128)S(1)} %collective-permute-done.4.first_top.first_end.first_ref, f32[2,32,2048]{2,1,0:T(8,128)S(1)} %shard_map.106.second_top.second_end.second_ref, f32[4,2048]{1,0:T(4,128)S(1)} %collective-permute-done.5.rim_ref, f32[9,96,32]{2,1,0:T(8,128)S(1)} %bitcast.19), custom_call_target="tpu_custom_call" | custom-call | flops 3623878656 | bytes 2097152 | tf_op jit(solution)/shard_map/pallas_call | solution.py:467
  173.5 2.8 %shard_map.109 = f32[64,2048]{1,0:T(8,128)} custom-call(f32[32,8,128]{2,1,0:T(8,128)S(1)} %all-to-all-done.3.own_ref, f32[32,8,128]{2,1,0:T(8,128)S(1)} %collective-permute-done.1.other_ref, bf16[2,2,2,128,64]{4,3,2,1,0:T(8,128)(2,1)S(1)} %copy-done.3, f32[2,16,128]{2,1,0:T(8,128)S(1)} %copy-done.7, f32[64,2048]{1,0:T(8,128)S(1)} %bitcast.14, ...), custom_call_target="tpu_custom_call" | custom-call | tf_op jit(solution)/shard_map/pallas_call | solution.py:560
  (22 shorter events, 0.2 us)
Async XLA Ops:
  0.0 1.0 copy-start.1
  1.0 0.9 copy-start.4
  2.0 101.5 %copy-start.2 = (f32[2,32,2048]{2,1,0:T(8,128)S(1)}, f32[2,32,2048]{2,1,0:T(8,128)}, u32[]{:S(2)}) copy-start(f32[2,32,2048]{2,1,0:T(8,128)} %first_ref) | copy-start | bytes 1572868
  2.0 124.3 %copy-start.5 = (bf16[2,256,128]{2,1,0:T(8,128)(2,1)S(1)}, bf16[2,256,128]{2,1,0:T(8,128)(2,1)}, u32[]{:S(2)}) copy-start(bf16[2,256,128]{2,1,0:T(8,128)(2,1)} %constant.12.clone.table_ref) | copy-start | bytes 393220
  2.0 135.6 %copy-start.8 = (f32[3,3,3,32,32]{4,3,2,1,0:T(8,128)S(1)}, f32[3,3,3,32,32]{4,3,2,1,0:T(8,128)}, u32[]{:S(2)}) copy-start(f32[3,3,3,32,32]{4,3,2,1,0:T(8,128)} %param.12) | copy-start | bytes 331780
  3.7 21.5 %collective-permute-start = (f32[32,8,128]{2,1,0:T(8,128)S(1)}, f32[32,8,128]{2,1,0:T(8,128)S(1)}, u32[]{:S(2)}, u32[]{:S(2)}) collective-permute-start(f32[32,8,128]{2,1,0:T(8,128)S(1)} %get-tuple-element.12), channel_id=1, source_target_pairs={{0,1},{1,0},{2,3},{3,2},{4,5},{5,4},{6,7},{7,6},{8,9},{9,8},{10,11... | collective-permute-start | bytes 393224 | tf_op jit(solution)/shard_map/ppermute | solution.py:524
  67.7 0.9 copy-start.6
  69.4 27.4 %all-to-all-start.1 = ((f32[32,4,128]{2,1,0:T(4,128)}), f32[32,4,128]{2,1,0:T(4,128)S(1)}, u32[]{:S(2)}, u32[]{:S(2)}) async-start(f32[32,4,128]{2,1,0:T(4,128)} %bitcast.2), calls=%async_computation.1 | async-start | bytes 131072 | tf_op jit(solution)/shard_map/all_to_all | solution.py:488
  74.2 3.4 %copy-start = (f32[16,1,16,2,32,32]{5,4,3,2,1,0:T(8,128)S(1)}, f32[16,1,16,2,32,32]{5,4,3,2,1,0:T(8,128)}, u32[]{:S(2)}) copy-start(f32[16,1,16,2,32,32]{5,4,3,2,1,0:T(8,128)} %param.11) | copy-start | bytes 6291460
  98.5 27.7 %all-to-all-start.2 = ((f32[32,4,128]{2,1,0:T(4,128)}), f32[32,4,128]{2,1,0:T(4,128)S(1)}, u32[]{:S(2)}, u32[]{:S(2)}) async-start(f32[32,4,128]{2,1,0:T(4,128)} %bitcast.5), calls=%async_computation.2 | async-start | bytes 131072 | tf_op jit(solution)/shard_map/all_to_all | solution.py:488
  103.5 28.4 %collective-permute-start.2 = (f32[2,32,2048]{2,1,0:T(8,128)S(1)}, f32[2,32,2048]{2,1,0:T(8,128)S(1)}, u32[]{:S(2)}, u32[]{:S(2)}) collective-permute-start(f32[2,32,2048]{2,1,0:T(8,128)S(1)} %copy-done.2), channel_id=1, source_target_pairs={{2,0},{4,2},{6,4},{8,6},{10,8},{12,10},{14,12},{16,14},{18,16},{20... | collective-permute-start | bytes 1572872 | tf_op jit(solution)/shard_map/ppermute | solution.py:528
  127.1 36.7 %all-to-all-start.3 = ((f32[32,8,128]{2,1,0:T(8,128)}), f32[32,8,128]{2,1,0:T(8,128)S(1)}, u32[]{:S(2)}, u32[]{:S(2)}) async-start(f32[32,8,128]{2,1,0:T(8,128)} %bitcast.7), calls=%async_computation.3 | async-start | bytes 262144 | tf_op jit(solution)/shard_map/all_to_all | solution.py:488
  131.8 31.9 %copy-start.10 = (f32[32]{0:T(128)S(1)}, f32[32]{0:T(128)}, u32[]{:S(2)}) copy-start(f32[32]{0:T(128)} %param.14) | copy-start | bytes 388
  131.9 32.7 %copy-start.9 = (f32[3,3,3,32,32]{4,3,2,1,0:T(8,128)S(1)}, f32[3,3,3,32,32]{4,3,2,1,0:T(8,128)}, u32[]{:S(2)}) copy-start(f32[3,3,3,32,32]{4,3,2,1,0:T(8,128)} %param.13) | copy-start | bytes 331780
  131.9 5.6 %collective-permute-start.3 = (f32[4,2048]{1,0:T(4,128)S(1)}, f32[4,2048]{1,0:T(4,128)S(1)}, u32[]{:S(2)}, u32[]{:S(2)}) collective-permute-start(f32[4,2048]{1,0:T(4,128)S(1)} %shard_map.105), channel_id=1, source_target_pairs={{0,1},{1,0},{2,3},{3,2},{4,5},{5,4},{6,7},{7,6},{8,9},{9,8},{10,11... | collective-permute-start | bytes 98312 | tf_op jit(solution)/shard_map/ppermute | solution.py:459
  146.5 27.0 %copy-start.3 = (bf16[2,2,2,128,64]{4,3,2,1,0:T(8,128)(2,1)S(1)}, bf16[2,2,2,128,64]{4,3,2,1,0:T(8,128)(2,1)}, u32[]{:S(2)}) copy-start(bf16[2,2,2,128,64]{4,3,2,1,0:T(8,128)(2,1)} %constant.13.clone.table_ref) | copy-start | bytes 393220
  146.5 27.0 %copy-start.7 = (f32[2,16,128]{2,1,0:T(8,128)S(1)}, f32[2,16,128]{2,1,0:T(8,128)}, u32[]{:S(2)}) copy-start(f32[2,16,128]{2,1,0:T(8,128)} %constant.14.clone.twiddle_ref) | copy-start | bytes 49156
  146.5 16.1 %collective-permute-start.4 = (f32[2,32,2048]{2,1,0:T(8,128)S(1)}, f32[2,32,2048]{2,1,0:T(8,128)S(1)}, u32[]{:S(2)}, u32[]{:S(2)}) collective-permute-start(f32[2,32,2048]{2,1,0:T(8,128)S(1)} %shard_map.106.second_top.second_end.second_ref), channel_id=1, source_target_pairs={{0,2},{2,4},{4,6},{6,8},{8,10},{10,12},{12,14},{14,16},{16,18},{18... | collective-permute-start | bytes 1572872 | tf_op jit(solution)/shard_map/ppermute | solution.py:553
  162.7 1.9 %collective-permute-start.5 = (f32[4,2048]{1,0:T(4,128)S(1)}, f32[4,2048]{1,0:T(4,128)S(1)}, u32[]{:S(2)}, u32[]{:S(2)}) collective-permute-start(f32[4,2048]{1,0:T(4,128)S(1)} %shard_map.107), channel_id=1, source_target_pairs={{0,1},{1,0},{2,3},{3,2},{4,5},{5,4},{6,7},{7,6},{8,9},{9,8},{10,11... | collective-permute-start | bytes 98312 | tf_op jit(solution)/shard_map/ppermute | solution.py:459
  163.8 9.7 %collective-permute-start.1 = (f32[32,8,128]{2,1,0:T(8,128)S(1)}, f32[32,8,128]{2,1,0:T(8,128)S(1)}, u32[]{:S(2)}, u32[]{:S(2)}) collective-permute-start(f32[32,8,128]{2,1,0:T(8,128)S(1)} %all-to-all-done.3.own_ref), channel_id=1, source_target_pairs={{0,1},{1,0},{2,3},{3,2},{4,5},{5,4},{6,7},{7,6},{8,9},{9,8},{10,11... | collective-permute-start | bytes 393224 | tf_op jit(solution)/shard_map/ppermute | solution.py:559

commit v4 on v3

--- a/solution.py
+++ b/solution.py
@@ -401,15 +401,12 @@
             outside = (at_start & (slot == 0)) | (at_end & (slot == 5))
         inside = jnp.where(outside, 0.0, 1.0)
         for shift in range(3):
-            for z in range(blocks):
-                value = pad_ref[
-                    x,
-                    TOP - 1 + shift : TOP - 1 + shift + cells_y,
-                    z * out_lanes : z * out_lanes + in_lanes,
-                ]
+            for z in range(pad_ref.shape[2] // out_lanes):
+                lanes = slice(z * out_lanes, (z + 1) * out_lanes)
+                value = pad_ref[x, TOP - 1 + shift : TOP - 1 + shift + cells_y, lanes]
                 high, low = split(value * inside)
-                high_ref[shift, z, slot] = high
-                low_ref[shift, z, slot] = low
+                high_ref[shift, slot, :, lanes] = high
+                low_ref[shift, slot, :, lanes] = low
         return carry
 
     lax.fori_loop(0, 3 * cells_x, fill, 0)
@@ -419,9 +416,21 @@
     def multiply(i, carry):
         shift_x = i // 3
         shift_y = i % 3
-        rows = blocks * cells_x * cells_y
-        high = high_ref[shift_y, :, pl.ds(shift_x * cells_x, cells_x)].reshape(rows, in_lanes)
-        low = low_ref[shift_y, :, pl.ds(shift_x * cells_x, cells_x)].reshape(rows, in_lanes)
+        high, low = (
+            jnp.concatenate(
+                [
+                    ref[
+                        shift_y,
+                        pl.ds(shift_x * cells_x, cells_x),
+                        :,
+                        z * out_lanes : z * out_lanes + in_lanes,
+                    ].reshape(cells_x * cells_y, in_lanes)
+                    for z in range(blocks)
+                ],
+                axis=0,
+            )
+            for ref in (high_ref, low_ref)
+        )
         table_high = table_high_ref[i]
         acc_ref[...] += dot(high, table_high) + (
             dot(high, table_low_ref[i]) + dot(low, table_high)
@@ -471,8 +480,8 @@
         out_specs=VMEM,
         scratch_shapes=[
             pltpu.VMEM((2 * cells_x, cells_y + 2 * TOP, width + 2 * LANES), F32),
-            pltpu.VMEM((3, blocks, 3 * cells_x, cells_y, WINDOW * CH), BF16),
-            pltpu.VMEM((3, blocks, 3 * cells_x, cells_y, WINDOW * CH), BF16),
+            pltpu.VMEM((3, 3 * cells_x, cells_y, width + 2 * LANES), BF16),
+            pltpu.VMEM((3, 3 * cells_x, cells_y, width + 2 * LANES), BF16),
             pltpu.VMEM((9, WINDOW * CH, BLOCK * CH), BF16),
             pltpu.VMEM((9, WINDOW * CH, BLOCK * CH), BF16),
             pltpu.VMEM((rows, BLOCK * CH), F32),

time: 177 us -> 177 us (level)
  no operation moved by 1% of the time
where the time goes in v4:
time: 177 us; the launch traced here: 176 us
  waiting for transfers between devices  54.6 us (31%)
  starting transfers between devices  44.1 us (25%)
  blocking collectives  42.4 us (24%)
  Pallas kernels  28.7 us (16%)
  local copies, waits for them, and re-layouts  6.36 us (4%)
    all_to_all x1, blocking collectives, all_to_all(): return lax.all_to_all(value, 'gx', split_axis=0, concat_axis=0, tiled=True)  42.4 us
    all_to_all x3, waiting for transfers between devices, all_to_all(): return lax.all_to_all(value, 'gx', split_axis=0, concat_axis=0, tiled=True)  36.8 us
    ppermute x1, starting transfers between devices, block(): lines = keep + lax.ppermute(send, 'gy', [(0, 1), (1, 0)])  20.5 us
    pallas_call x2, Pallas kernels, band_product(): pl.pallas_call(functools.partial(conv_kernel, shifted=shifted, activate=a...  17.8 us
    ppermute x1, waiting for transfers between devices, block(): lax.ppermute(hidden, 'gx', [(i, (i + 1) % devices_x) for i in range(devic...  15.2 us
    all_to_all x3, starting transfers between devices, all_to_all(): return lax.all_to_all(value, 'gx', split_axis=0, concat_axis=0, tiled=True)  14.5 us
    unnamed x22, local copies, waits for them, and re-layouts  6.27 us
    ppermute x2, starting transfers between devices, convolve(): rim = lax.ppermute(rim, 'gy', [(0, 1), (1, 0)])  5.77 us
  transfers between devices with their start and end apart: 9, of which 6 were waited for; matrix products, arithmetic and copies ran while one was open for 0% of the time, Pallas kernels for 12%

profile of v4, /device:TPU:37, one launch (start us, length us, event | category | flops | bytes accessed | tf_op | source)
XLA Modules:
  0.0 176.3 jit_solution(6876155788736027980)
XLA Ops:
  0.0 1.0 copy-done.1
  1.0 0.9 copy-done.4
  2.0 1.7 shard_map.100
  3.7 20.5 %collective-permute-start = (f32[32,8,128]{2,1,0:T(8,128)S(1)}, f32[32,8,128]{2,1,0:T(8,128)S(1)}, u32[]{:S(2)}, u32[]{:S(2)}) collective-permute-start(f32[32,8,128]{2,1,0:T(8,128)S(1)} %get-tuple-element.12), channel_id=1, source_target_pairs={{0,1},{1,0},{2,3},{3,2},{4,5},{5,4},{6,7},{7,6},{8,9},{9,8},{10,11... | collective-permute-start | bytes 393224 | tf_op jit(solution)/shard_map/ppermute | solution.py:533
  24.3 1.0 collective-permute-done
  25.3 42.4 %all_to_all.20 = f32[32,8,128]{2,1,0:T(8,128)S(1)} all-to-all(f32[32,8,128]{2,1,0:T(8,128)S(1)} %add.3), channel_id=1, replica_groups=mesh['groups'=4,'gx'=32,'gy'=2] {'gx'}, dimensions={0} | all-to-all | bytes 262144 | tf_op jit(solution)/shard_map/all_to_all | solution.py:497
  67.7 0.9 copy-done.6
  68.6 0.8 shard_map.101
  69.4 4.8 %all-to-all-start.1 = ((f32[32,4,128]{2,1,0:T(4,128)}), f32[32,4,128]{2,1,0:T(4,128)S(1)}, u32[]{:S(2)}, u32[]{:S(2)}) async-start(f32[32,4,128]{2,1,0:T(4,128)} %bitcast.2), calls=%async_computation.1 | async-start | bytes 131072 | tf_op jit(solution)/shard_map/all_to_all | solution.py:497
  74.2 3.4 %copy-done = f32[16,1,16,2,32,32]{5,4,3,2,1,0:T(8,128)S(1)} copy-done((f32[16,1,16,2,32,32]{5,4,3,2,1,0:T(8,128)S(1)}, f32[16,1,16,2,32,32]{5,4,3,2,1,0:T(8,128)}, u32[]{:S(2)}) %copy-start) | copy-done | bytes 2097176
  77.5 2.8 %shard_map.102 = (bf16[4,16,64,128]{3,2,1,0:T(8,128)(2,1)S(1)}, bf16[4,16,64,128]{3,2,1,0:T(8,128)(2,1)S(1)}) custom-call(f32[16,1024,32]{2,1,0:T(8,128)S(1)} %bitcast.12), custom_call_target="tpu_custom_call" | custom-call | flops 268435456 | bytes 16777216 | tf_op jit(solution)/shard_map/pallas_call | solution.py:546
  80.3 16.5 %all-to-all-done.1 = f32[32,4,128]{2,1,0:T(4,128)S(1)} async-done(((f32[32,4,128]{2,1,0:T(4,128)}), f32[32,4,128]{2,1,0:T(4,128)S(1)}, u32[]{:S(2)}, u32[]{:S(2)}) %all-to-all-start.1) | async-done | bytes 65568 | tf_op jit(solution)/shard_map/all_to_all | solution.py:497
  96.8 1.8 shard_map.103
  98.5 5.0 %all-to-all-start.2 = ((f32[32,4,128]{2,1,0:T(4,128)}), f32[32,4,128]{2,1,0:T(4,128)S(1)}, u32[]{:S(2)}, u32[]{:S(2)}) async-start(f32[32,4,128]{2,1,0:T(4,128)} %bitcast.5), calls=%async_computation.2 | async-start | bytes 131072 | tf_op jit(solution)/shard_map/all_to_all | solution.py:497
  103.5 2.3 %collective-permute-start.2 = (f32[2,32,2048]{2,1,0:T(8,128)S(1)}, f32[2,32,2048]{2,1,0:T(8,128)S(1)}, u32[]{:S(2)}, u32[]{:S(2)}) collective-permute-start(f32[2,32,2048]{2,1,0:T(8,128)S(1)} %copy-done.2), channel_id=1, source_target_pairs={{2,0},{4,2},{6,4},{8,6},{10,8},{12,10},{14,12},{16,14},{18,16},{20... | collective-permute-start | bytes 1572872 | tf_op jit(solution)/shard_map/ppermute | solution.py:537
  105.9 20.4 %all-to-all-done.2 = f32[32,4,128]{2,1,0:T(4,128)S(1)} async-done(((f32[32,4,128]{2,1,0:T(4,128)}), f32[32,4,128]{2,1,0:T(4,128)S(1)}, u32[]{:S(2)}, u32[]{:S(2)}) %all-to-all-start.2) | async-done | bytes 65568 | tf_op jit(solution)/shard_map/all_to_all | solution.py:497
  126.2 0.9 shard_map.104
  127.1 4.8 %all-to-all-start.3 = ((f32[32,8,128]{2,1,0:T(8,128)}), f32[32,8,128]{2,1,0:T(8,128)S(1)}, u32[]{:S(2)}, u32[]{:S(2)}) async-start(f32[32,8,128]{2,1,0:T(8,128)} %bitcast.7), calls=%async_computation.3 | async-start | bytes 262144 | tf_op jit(solution)/shard_map/all_to_all | solution.py:497
  131.8 0.0 copy-start.10
  131.9 4.7 %collective-permute-start.3 = (f32[4,2048]{1,0:T(4,128)S(1)}, f32[4,2048]{1,0:T(4,128)S(1)}, u32[]{:S(2)}, u32[]{:S(2)}) collective-permute-start(f32[4,2048]{1,0:T(4,128)S(1)} %shard_map.105), channel_id=1, source_target_pairs={{0,1},{1,0},{2,3},{3,2},{4,5},{5,4},{6,7},{7,6},{8,9},{9,8},{10,11... | collective-permute-start | bytes 98312 | tf_op jit(solution)/shard_map/ppermute | solution.py:468
  136.7 0.9 collective-permute-done.3.rim_ref
  137.5 8.9 %shard_map.106.second_top.second_end.second_ref = f32[2,32,2048]{2,1,0:T(8,128)S(1)} custom-call(f32[2,32,2048]{2,1,0:T(8,128)S(1)} %copy-done.2, f32[2,32,2048]{2,1,0:T(8,128)S(1)} %collective-permute-done.2.second_top.second_end.second_ref, f32[4,2048]{1,0:T(4,128)S(1)} %collective-permute-done.3.rim_ref, f32[9,96,32]{2,1,0:T(8,128)S(1)} %bitcast.18), custom_call_target="tpu_custom_call" | custom-call | flops 3623878656 | bytes 2097152 | tf_op jit(solution)/shard_map/pallas_call | solution.py:476
  146.5 0.0 copy-start.3
  146.5 0.0 copy-start.7
  146.5 0.9 collective-permute-start.4
  147.3 15.2 %collective-permute-done.4.first_top.first_end.first_ref = f32[2,32,2048]{2,1,0:T(8,128)S(1)} collective-permute-done((f32[2,32,2048]{2,1,0:T(8,128)S(1)}, f32[2,32,2048]{2,1,0:T(8,128)S(1)}, u32[]{:S(2)}, u32[]{:S(2)}) %collective-permute-start.4) | collective-permute-done | bytes 524320 | tf_op jit(solution)/shard_map/ppermute | solution.py:562
  162.6 1.0 collective-permute-start.5
  163.7 0.1 reshape_tile.3.bias_ref
  163.8 0.1 collective-permute-start.1
  163.9 0.7 collective-permute-done.5.rim_ref
  164.5 8.9 %shard_map.108 = f32[2,32,2048]{2,1,0:T(8,128)S(1)} custom-call(f32[2,32,2048]{2,1,0:T(8,128)S(1)} %collective-permute-done.4.first_top.first_end.first_ref, f32[2,32,2048]{2,1,0:T(8,128)S(1)} %shard_map.106.second_top.second_end.second_ref, f32[4,2048]{1,0:T(4,128)S(1)} %collective-permute-done.5.rim_ref, f32[9,96,32]{2,1,0:T(8,128)S(1)} %bitcast.19), custom_call_target="tpu_custom_call" | custom-call | flops 3623878656 | bytes 2097152 | tf_op jit(solution)/shard_map/pallas_call | solution.py:476
  173.5 2.8 %shard_map.109 = f32[64,2048]{1,0:T(8,128)} custom-call(f32[32,8,128]{2,1,0:T(8,128)S(1)} %all-to-all-done.3.own_ref, f32[32,8,128]{2,1,0:T(8,128)S(1)} %collective-permute-done.1.other_ref, bf16[2,2,2,128,64]{4,3,2,1,0:T(8,128)(2,1)S(1)} %copy-done.3, f32[2,16,128]{2,1,0:T(8,128)S(1)} %copy-done.7, f32[64,2048]{1,0:T(8,128)S(1)} %bitcast.14, ...), custom_call_target="tpu_custom_call" | custom-call | tf_op jit(solution)/shard_map/pallas_call | solution.py:569
  (22 shorter events, 0.2 us)
Async XLA Ops:
  0.0 1.0 copy-start.1
  1.0 0.9 copy-start.4
  2.0 101.5 %copy-start.2 = (f32[2,32,2048]{2,1,0:T(8,128)S(1)}, f32[2,32,2048]{2,1,0:T(8,128)}, u32[]{:S(2)}) copy-start(f32[2,32,2048]{2,1,0:T(8,128)} %first_ref) | copy-start | bytes 1572868
  2.0 124.3 %copy-start.5 = (bf16[2,256,128]{2,1,0:T(8,128)(2,1)S(1)}, bf16[2,256,128]{2,1,0:T(8,128)(2,1)}, u32[]{:S(2)}) copy-start(bf16[2,256,128]{2,1,0:T(8,128)(2,1)} %constant.12.clone.table_ref) | copy-start | bytes 393220
  2.0 135.6 %copy-start.8 = (f32[3,3,3,32,32]{4,3,2,1,0:T(8,128)S(1)}, f32[3,3,3,32,32]{4,3,2,1,0:T(8,128)}, u32[]{:S(2)}) copy-start(f32[3,3,3,32,32]{4,3,2,1,0:T(8,128)} %param.12) | copy-start | bytes 331780
  3.7 21.5 %collective-permute-start = (f32[32,8,128]{2,1,0:T(8,128)S(1)}, f32[32,8,128]{2,1,0:T(8,128)S(1)}, u32[]{:S(2)}, u32[]{:S(2)}) collective-permute-start(f32[32,8,128]{2,1,0:T(8,128)S(1)} %get-tuple-element.12), channel_id=1, source_target_pairs={{0,1},{1,0},{2,3},{3,2},{4,5},{5,4},{6,7},{7,6},{8,9},{9,8},{10,11... | collective-permute-start | bytes 393224 | tf_op jit(solution)/shard_map/ppermute | solution.py:533
  67.7 0.9 copy-start.6
  69.4 27.4 %all-to-all-start.1 = ((f32[32,4,128]{2,1,0:T(4,128)}), f32[32,4,128]{2,1,0:T(4,128)S(1)}, u32[]{:S(2)}, u32[]{:S(2)}) async-start(f32[32,4,128]{2,1,0:T(4,128)} %bitcast.2), calls=%async_computation.1 | async-start | bytes 131072 | tf_op jit(solution)/shard_map/all_to_all | solution.py:497
  74.2 3.4 %copy-start = (f32[16,1,16,2,32,32]{5,4,3,2,1,0:T(8,128)S(1)}, f32[16,1,16,2,32,32]{5,4,3,2,1,0:T(8,128)}, u32[]{:S(2)}) copy-start(f32[16,1,16,2,32,32]{5,4,3,2,1,0:T(8,128)} %param.11) | copy-start | bytes 6291460
  98.5 27.7 %all-to-all-start.2 = ((f32[32,4,128]{2,1,0:T(4,128)}), f32[32,4,128]{2,1,0:T(4,128)S(1)}, u32[]{:S(2)}, u32[]{:S(2)}) async-start(f32[32,4,128]{2,1,0:T(4,128)} %bitcast.5), calls=%async_computation.2 | async-start | bytes 131072 | tf_op jit(solution)/shard_map/all_to_all | solution.py:497
  103.5 28.4 %collective-permute-start.2 = (f32[2,32,2048]{2,1,0:T(8,128)S(1)}, f32[2,32,2048]{2,1,0:T(8,128)S(1)}, u32[]{:S(2)}, u32[]{:S(2)}) collective-permute-start(f32[2,32,2048]{2,1,0:T(8,128)S(1)} %copy-done.2), channel_id=1, source_target_pairs={{2,0},{4,2},{6,4},{8,6},{10,8},{12,10},{14,12},{16,14},{18,16},{20... | collective-permute-start | bytes 1572872 | tf_op jit(solution)/shard_map/ppermute | solution.py:537
  127.1 36.7 %all-to-all-start.3 = ((f32[32,8,128]{2,1,0:T(8,128)}), f32[32,8,128]{2,1,0:T(8,128)S(1)}, u32[]{:S(2)}, u32[]{:S(2)}) async-start(f32[32,8,128]{2,1,0:T(8,128)} %bitcast.7), calls=%async_computation.3 | async-start | bytes 262144 | tf_op jit(solution)/shard_map/all_to_all | solution.py:497
  131.8 31.8 %copy-start.10 = (f32[32]{0:T(128)S(1)}, f32[32]{0:T(128)}, u32[]{:S(2)}) copy-start(f32[32]{0:T(128)} %param.14) | copy-start | bytes 388
  131.9 32.7 %copy-start.9 = (f32[3,3,3,32,32]{4,3,2,1,0:T(8,128)S(1)}, f32[3,3,3,32,32]{4,3,2,1,0:T(8,128)}, u32[]{:S(2)}) copy-start(f32[3,3,3,32,32]{4,3,2,1,0:T(8,128)} %param.13) | copy-start | bytes 331780
  131.9 5.6 %collective-permute-start.3 = (f32[4,2048]{1,0:T(4,128)S(1)}, f32[4,2048]{1,0:T(4,128)S(1)}, u32[]{:S(2)}, u32[]{:S(2)}) collective-permute-start(f32[4,2048]{1,0:T(4,128)S(1)} %shard_map.105), channel_id=1, source_target_pairs={{0,1},{1,0},{2,3},{3,2},{4,5},{5,4},{6,7},{7,6},{8,9},{9,8},{10,11... | collective-permute-start | bytes 98312 | tf_op jit(solution)/shard_map/ppermute | solution.py:468
  146.5 27.0 %copy-start.3 = (bf16[2,2,2,128,64]{4,3,2,1,0:T(8,128)(2,1)S(1)}, bf16[2,2,2,128,64]{4,3,2,1,0:T(8,128)(2,1)}, u32[]{:S(2)}) copy-start(bf16[2,2,2,128,64]{4,3,2,1,0:T(8,128)(2,1)} %constant.13.clone.table_ref) | copy-start | bytes 393220
  146.5 27.0 %copy-start.7 = (f32[2,16,128]{2,1,0:T(8,128)S(1)}, f32[2,16,128]{2,1,0:T(8,128)}, u32[]{:S(2)}) copy-start(f32[2,16,128]{2,1,0:T(8,128)} %constant.14.clone.twiddle_ref) | copy-start | bytes 49156
  146.5 16.1 %collective-permute-start.4 = (f32[2,32,2048]{2,1,0:T(8,128)S(1)}, f32[2,32,2048]{2,1,0:T(8,128)S(1)}, u32[]{:S(2)}, u32[]{:S(2)}) collective-permute-start(f32[2,32,2048]{2,1,0:T(8,128)S(1)} %shard_map.106.second_top.second_end.second_ref), channel_id=1, source_target_pairs={{0,2},{2,4},{4,6},{6,8},{8,10},{10,12},{12,14},{14,16},{16,18},{18... | collective-permute-start | bytes 1572872 | tf_op jit(solution)/shard_map/ppermute | solution.py:562
  162.6 1.9 %collective-permute-start.5 = (f32[4,2048]{1,0:T(4,128)S(1)}, f32[4,2048]{1,0:T(4,128)S(1)}, u32[]{:S(2)}, u32[]{:S(2)}) collective-permute-start(f32[4,2048]{1,0:T(4,128)S(1)} %shard_map.107), channel_id=1, source_target_pairs={{0,1},{1,0},{2,3},{3,2},{4,5},{5,4},{6,7},{7,6},{8,9},{9,8},{10,11... | collective-permute-start | bytes 98312 | tf_op jit(solution)/shard_map/ppermute | solution.py:468
  163.8 9.7 %collective-permute-start.1 = (f32[32,8,128]{2,1,0:T(8,128)S(1)}, f32[32,8,128]{2,1,0:T(8,128)S(1)}, u32[]{:S(2)}, u32[]{:S(2)}) collective-permute-start(f32[32,8,128]{2,1,0:T(8,128)S(1)} %all-to-all-done.3.own_ref), channel_id=1, source_target_pairs={{0,1},{1,0},{2,3},{3,2},{4,5},{5,4},{6,7},{7,6},{8,9},{9,8},{10,11... | collective-permute-start | bytes 393224 | tf_op jit(solution)/shard_map/ppermute | solution.py:568
